TPU v7x, 32 devices: a whole 2x2x4 slice. The times are simulated.
32 devices in a mesh: group: 8 (over z, x), tensor: 4 (over y, core).
Axes of the slice: x: 2, y: 2, z: 4, core: 2. Of those that a mesh axis runs over, the one named last changes fastest.
Arguments:
- queries: bfloat16 [1024, 4096], P('group', 'tensor'), may hold values from -120 to 120
- keys: bfloat16 [1024, 512], P('group', 'tensor'), may hold values from -6 to 6
- values: bfloat16 [1024, 512], P('group', 'tensor'), may hold values from -6 to 6
- document_index: int32 [8, 128], P('group'), may hold values from 0 to 7, never falling along the last dimension, each value on 1 to 64 neighbouring positions
- out_proj: bfloat16 [4096, 4096], P('tensor', 'group'), may hold values from -0.25 to 0.25
- residual_in: bfloat16 [1024, 4096], P(('group', 'tensor')), may hold values from -60 to 60
- norm_gain: float32 [4096], replicated, may hold values from 0.1 to 1.9
- expert_ids: int32 [1024, 8], P(('group', 'tensor')), may hold values from 0 to 31, all different within a row; in each aligned block of 32 rows (0 to 31, 32 to 63, ...) at most 16 rows name the same one
- gate_weights: float32 [1024, 8], P(('group', 'tensor')), may hold values from 0.05 to 0.45
- w_gate_up: bfloat16 [32, 4096, 1536], P(('group', 'tensor')), may hold values from -0.09375 to 0.09375
- w_down: bfloat16 [32, 768, 4096], P(('group', 'tensor')), may hold values from -0.21875 to 0.21875
Outputs:
- layer_out: bfloat16 [1024, 4096], P(('group', 'tensor'))
Inputs may be any that keep to these rules, and one draw needn't show every extreme that they name: `document_index`: ids never fall along a group's tokens; equal ids mark one document. `expert_ids`: a token names 8 different experts; among the 32 tokens of one device (aligned blocks of rows) no expert is named more than 16 times, a bound that some block reaches.
All inputs are finite; a program needn't handle non-finite values.
Results may differ from a plain program's by a relative error of at most 0.0045.
Values may be sent and summed in bfloat16 or wider, within the bound.
A program may use at most 128 MiB of HBM per device.

v0:
```python
import functools

import jax
import jax.numpy as jnp
from jax import lax
from jax.experimental import pallas as pl
from jax.experimental.pallas import tpu as pltpu
from jax.sharding import PartitionSpec as P

HEAD_SIZE = 128
LANES = 128


def attention(queries, keys, values, document_index):
    token_group = queries.shape[0]
    kv_dev = keys.shape[1] // HEAD_SIZE
    query_dev = queries.shape[1] // HEAD_SIZE
    group_ratio = query_dev // kv_dev
    query_head_split = queries.reshape(token_group, kv_dev, group_ratio, HEAD_SIZE)
    key_head_split = keys.reshape(token_group, kv_dev, HEAD_SIZE)
    value_head_split = values.reshape(token_group, kv_dev, HEAD_SIZE)
    scores = jnp.einsum(
        "qgrd,kgd->grqk", query_head_split, key_head_split, preferred_element_type=jnp.float32
    ) * (1.0 / HEAD_SIZE**0.5)
    doc_row = document_index[0]
    positions = jnp.arange(token_group, dtype=jnp.int32)
    visible = (positions[:, None] >= positions[None, :]) & (doc_row[:, None] == doc_row[None, :])
    scores = jnp.where(visible, scores, -jnp.inf)
    row_max = jnp.max(scores, axis=-1, keepdims=True)
    exponent = jnp.where(visible, jnp.exp(scores - row_max), 0.0)
    weights = (exponent / jnp.sum(exponent, axis=-1, keepdims=True)).astype(jnp.bfloat16)
    head_out = jnp.einsum(
        "grqk,kgd->qgrd", weights, value_head_split, preferred_element_type=jnp.float32
    )
    return head_out.astype(jnp.bfloat16).reshape(token_group, query_dev * HEAD_SIZE)


MESH = pl.DeviceIdType.MESH
VMEM_LIMIT = 60 * 1024 * 1024


def place(sizes):
    g, t = lax.axis_index("group"), lax.axis_index("tensor")
    return g // 2, g % 2, t // 2, t % 2


def device(z, x, y, c):
    return (z * 2 + x, y * 2 + c)


def enter(partners):
    barrier = pltpu.get_barrier_semaphore()
    for partner in partners:
        pl.semaphore_signal(barrier, inc=1, device_id=partner, device_id_type=MESH)
    pl.semaphore_wait(barrier, len(partners))


def remote(src, dst, send, recv, target):
    return pltpu.make_async_remote_copy(
        src_ref=src,
        dst_ref=dst,
        send_sem=send,
        recv_sem=recv,
        device_id=target,
        device_id_type=MESH,
    )


def project_kernel(
    slabs,
    head_ref,
    w_ref,
    out_ref,
    heads,
    part,
    got_core,
    sum_core,
    got_y,
    sum_y,
    landed,
    z_send,
    z_recv,
    x_send,
    x_recv,
    c_send,
    c_recv,
    y_send,
    y_recv,
    o_send,
    o_recv,
):
    z, x, y, c = place(None)
    width = w_ref.shape[1]
    tok = out_ref.shape[0]
    after = [lax.rem(z + j, slabs) for j in range(slabs)]
    before = [lax.rem(z + slabs - j, slabs) for j in range(slabs)]
    core, over_y, over_x = device(z, x, y, 1 - c), device(z, x, 1 - y, c), device(z, 1 - x, y, c)
    enter(
        [core, over_y]
        + [device(after[j], x, y, c) for j in range(1, slabs)]
        + [device(after[j], 1 - x, y, c) for j in range(slabs)]
    )
    pending = []

    def start(copy):
        copy.start()
        pending.append(copy)
        return copy

    z_copy = [None] * slabs
    x_copy = [None] * slabs
    x_copy[0] = start(remote(head_ref, heads.at[0, 1], x_send.at[0], x_recv.at[0], over_x))
    for j in range(1, slabs):
        z_copy[j] = start(
            remote(
                head_ref, heads.at[j, 0], z_send.at[j], z_recv.at[j], device(before[j], x, y, c)
            )
        )
    c_copy, y_copy, o_copy = [None] * slabs, [None] * slabs, []

    def project(j):
        for side in range(2):
            rows = head_ref if j == 0 and side == 0 else heads.at[j, side]
            got = jnp.dot(rows[...], w_ref[...], preferred_element_type=jnp.float32)
            part[j, :, side] = got.reshape(2, 2, tok, width).transpose(1, 0, 2, 3)
        c_copy[j] = start(
            remote(part.at[j, 1 - c], got_core.at[j], c_send.at[j], c_recv.at[j], core)
        )

    def over_cores(j):
        c_copy[j].wait_recv()
        for side in range(2):
            for row in range(2):
                sum_core[j, row, side] = part[j, c, side, row] + got_core[j, side, row]
        y_copy[j] = start(
            remote(sum_core.at[j, 1 - y], got_y.at[j], y_send.at[j], y_recv.at[j], over_y)
        )

    def over_rows(j):
        y_copy[j].wait_recv()
        for side in range(2):
            total = (sum_core[j, y, side] + got_y[j, side]).astype(jnp.bfloat16)
            if j == 0 and side == 0:
                landed[0, 0] = total
                continue
            sum_y[j, side] = total
            target = device(after[j], x if side == 0 else 1 - x, y, c)
            o_copy.append(
                start(
                    remote(
                        sum_y.at[j, side],
                        landed.at[j, side],
                        o_send.at[j, side],
                        o_recv.at[j, side],
                        target,
                    )
                )
            )

    for j in range(slabs):
        if j + 1 < slabs:
            z_copy[j + 1].wait_recv()
            x_copy[j + 1] = start(
                remote(
                    heads.at[j + 1, 0],
                    heads.at[j + 1, 1],
                    x_send.at[j + 1],
                    x_recv.at[j + 1],
                    over_x,
                )
            )
        x_copy[j].wait_recv()
        project(j)
        if j >= 1:
            over_cores(j - 1)
        if j >= 2:
            over_rows(j - 2)
    over_cores(slabs - 1)
    for j in range(max(slabs - 2, 0), slabs):
        over_rows(j)
    for copy in o_copy:
        copy.wait_recv()
    for copy in pending:
        copy.wait_send()
    for j in range(slabs):
        for side in range(2):
            owner = before[j] * 2 + (x if side == 0 else 1 - x)
            columns = pl.ds(pl.multiple_of(owner * width, width), width)
            out_ref[:, columns] = landed[j, side].astype(jnp.float32)


def project(head_out, out_proj, groups, tok_dev):
    slabs = groups // 2
    tokens, depth = head_out.shape
    width = out_proj.shape[1]
    dma = pltpu.SemaphoreType.DMA
    return pl.pallas_call(
        functools.partial(project_kernel, slabs),
        out_shape=jax.ShapeDtypeStruct((tok_dev, groups * width), jnp.float32),
        in_specs=[pl.BlockSpec(memory_space=pltpu.VMEM)] * 2,
        out_specs=pl.BlockSpec(memory_space=pltpu.VMEM),
        scratch_shapes=[
            pltpu.VMEM((slabs, 2, tokens, depth), jnp.bfloat16),
            pltpu.VMEM((slabs, 2, 2, 2, tok_dev, width), jnp.float32),
            pltpu.VMEM((slabs, 2, 2, tok_dev, width), jnp.float32),
            pltpu.VMEM((slabs, 2, 2, tok_dev, width), jnp.float32),
            pltpu.VMEM((slabs, 2, tok_dev, width), jnp.float32),
            pltpu.VMEM((slabs, 2, tok_dev, width), jnp.bfloat16),
            pltpu.VMEM((slabs, 2, tok_dev, width), jnp.bfloat16),
        ]
        + [dma((slabs,))] * 8
        + [dma((slabs, 2))] * 2,
        compiler_params=pltpu.CompilerParams(
            collective_id=0, has_side_effects=True, vmem_limit_bytes=VMEM_LIMIT
        ),
    )(head_out, out_proj)


def combine_kernel(
    slabs,
    w_ref,
    hidden_ref,
    out_ref,
    got_core,
    sum_core,
    got_a,
    got_b,
    sum_a,
    sum_b,
    last_a,
    last_b,
    done,
    landed,
    c_send,
    c_recv,
    a_send,
    a_recv,
    b_send,
    b_recv,
    la_send,
    la_recv,
    lb_send,
    lb_recv,
    z_send,
    z_recv,
):
    z, x, y, c = place(None)
    tok, width = out_ref.shape
    half = width // 2
    step = 512
    after = [lax.rem(z + j, slabs) for j in range(slabs)]
    core, over_y, over_x = device(z, x, y, 1 - c), device(z, x, 1 - y, c), device(z, 1 - x, y, c)
    enter([core, over_y, over_x] + [device(after[j], x, y, c) for j in range(1, slabs)])
    pending = []

    def start(copy):
        copy.start()
        pending.append(copy)
        return copy

    order = [j for j in range(1, slabs)] + [0]
    c_copy = {
        j: start(
            remote(
                w_ref.at[after[j], :, :, 1 - c],
                got_core.at[j],
                c_send.at[j],
                c_recv.at[j],
                core,
            )
        )
        for j in order
    }
    a_copy, b_copy, la_copy, lb_copy, z_copy = {}, {}, {}, {}, {}

    def add(n, first, second, store):
        @pl.loop(0, n // step)
        def _(i):
            columns = pl.ds(pl.multiple_of(i * step, step), step)
            store(columns, first(columns).astype(jnp.float32) + second(columns).astype(jnp.float32))

    def over_cores(j):
        c_copy[j].wait_recv()
        for u in range(2):
            for v in range(2):

                def store(columns, value):
                    sum_core[j, u, v, :, columns] = value.astype(jnp.bfloat16)

                add(
                    width,
                    lambda columns: w_ref[after[j], u, v, c, :, columns],
                    lambda columns: got_core[j, u, v, :, columns],
                    store,
                )
        a_copy[j] = start(
            remote(
                sum_core.at[j, 1 - x, :, :, pl.ds(0, half)],
                got_a.at[j],
                a_send.at[j],
                a_recv.at[j],
                over_x,
            )
        )
        b_copy[j] = start(
            remote(
                sum_core.at[j, :, 1 - y, :, pl.ds(half, half)],
                got_b.at[j],
                b_send.at[j],
                b_recv.at[j],
                over_y,
            )
        )

    def second(j):
        a_copy[j].wait_recv()
        b_copy[j].wait_recv()
        for v in range(2):

            def store_a(columns, value):
                sum_a[j, v, :, columns] = value.astype(jnp.bfloat16)

            add(
                half,
                lambda columns: sum_core[j, x, v, :, columns],
                lambda columns: got_a[j, v, :, columns],
                store_a,
            )

            def store_b(columns, value):
                sum_b[j, v, :, columns] = value.astype(jnp.bfloat16)

            add(
                half,
                lambda columns: sum_core[
                    j, v, y, :, pl.ds(pl.multiple_of(columns.start + half, step), step)
                ],
                lambda columns: got_b[j, v, :, columns],
                store_b,
            )
        la_copy[j] = start(
            remote(sum_a.at[j, 1 - y], last_a.at[j], la_send.at[j], la_recv.at[j], over_y)
        )
        lb_copy[j] = start(
            remote(sum_b.at[j, 1 - x], last_b.at[j], lb_send.at[j], lb_recv.at[j], over_x)
        )

    def third(j):
        la_copy[j].wait_recv()
        lb_copy[j].wait_recv()

        def store_a(columns, value):
            done[j, :, columns] = value.astype(jnp.bfloat16)

        add(
            half,
            lambda columns: sum_a[j, y, :, columns],
            lambda columns: last_a[j, :, columns],
            store_a,
        )

        def store_b(columns, value):
            shifted = pl.ds(pl.multiple_of(columns.start + half, step), step)
            done[j, :, shifted] = value.astype(jnp.bfloat16)

        add(
            half,
            lambda columns: sum_b[j, x, :, columns],
            lambda columns: last_b[j, :, columns],
            store_b,
        )
        if j:
            z_copy[j] = start(
                remote(
                    done.at[j],
                    landed.at[j],
                    z_send.at[j],
                    z_recv.at[j],
                    device(after[j], x, y, c),
                )
            )

    for i, j in enumerate(order):
        over_cores(j)
        if i >= 1:
            second(order[i - 1])
        if i >= 2:
            third(order[i - 2])
    second(order[-1])
    for j in order[max(slabs - 2, 0) :]:
        third(j)
    for j in range(1, slabs):
        z_copy[j].wait_recv()
    for copy in pending:
        copy.wait_send()

    @pl.loop(0, width // step)
    def _(i):
        columns = pl.ds(pl.multiple_of(i * step, step), step)
        total = hidden_ref[:, columns] + done[0, :, columns].astype(jnp.float32)
        for j in range(1, slabs):
            total = total + landed[j, :, columns].astype(jnp.float32)
        out_ref[:, columns] = total.astype(jnp.bfloat16)


def combine(weighted, hidden, groups):
    slabs = groups // 2
    tok, width = hidden.shape
    half = width // 2
    dma = pltpu.SemaphoreType.DMA
    bf16 = jnp.bfloat16
    return pl.pallas_call(
        functools.partial(combine_kernel, slabs),
        out_shape=jax.ShapeDtypeStruct((tok, width), bf16),
        in_specs=[pl.BlockSpec(memory_space=pltpu.VMEM)] * 2,
        out_specs=pl.BlockSpec(memory_space=pltpu.VMEM),
        scratch_shapes=[
            pltpu.VMEM((slabs, 2, 2, tok, width), bf16),
            pltpu.VMEM((slabs, 2, 2, tok, width), bf16),
            pltpu.VMEM((slabs, 2, tok, half), bf16),
            pltpu.VMEM((slabs, 2, tok, half), bf16),
            pltpu.VMEM((slabs, 2, tok, half), bf16),
            pltpu.VMEM((slabs, 2, tok, half), bf16),
            pltpu.VMEM((slabs, tok, half), bf16),
            pltpu.VMEM((slabs, tok, half), bf16),
            pltpu.VMEM((slabs, tok, width), bf16),
            pltpu.VMEM((slabs, tok, width), bf16),
        ]
        + [dma((slabs,))] * 12,
        compiler_params=pltpu.CompilerParams(
            collective_id=1, has_side_effects=True, vmem_limit_bytes=VMEM_LIMIT
        ),
    )(weighted.reshape(slabs, 2, 2, 2, tok, width), hidden)


def gather_kernel(slabs, half, rows_ref, out_ref, own_sem, *sems):
    z, x, y, c = place(None)
    width = rows_ref.shape[1]
    low, high = pl.ds(0, half), pl.ds(half, width - half)
    after = [lax.rem(z + j, slabs) for j in range(slabs)]
    before = [lax.rem(z + slabs - j, slabs) for j in range(slabs)]
    core, over_y, over_x = device(z, x, y, 1 - c), device(z, x, 1 - y, c), device(z, 1 - x, y, c)
    own = pltpu.make_async_copy(rows_ref, out_ref.at[z, x, y, c], own_sem)
    own.start()
    enter([core, over_y, over_x] + [device(after[j], x, y, c) for j in range(1, slabs)])
    copies = {}

    def send(kind, j, src, dst, target):
        copy = remote(src, dst, sems[2 * kind].at[j], sems[2 * kind + 1].at[j], target)
        copy.start()
        copies[kind, j] = copy

    def pass_on(kind, j, block, target):
        send(kind, j, block, block, target)

    for j in range(1, slabs):
        send(0, j, rows_ref, out_ref.at[z, x, y, c], device(before[j], x, y, c))

    def first(j):
        if j:
            copies[0, j].wait_recv()
        else:
            own.wait()
        pass_on(1, j, out_ref.at[after[j], x, y, c, :, low], over_x)
        pass_on(2, j, out_ref.at[after[j], x, y, c, :, high], over_y)
        pass_on(3, j, out_ref.at[after[j], x, y, c], core)

    def second(j):
        copies[1, j].wait_recv()
        pass_on(4, j, out_ref.at[after[j], :, y, c, :, low], over_y)
        pass_on(5, j, out_ref.at[after[j], 1 - x, y, c, :, low], core)
        copies[2, j].wait_recv()
        pass_on(6, j, out_ref.at[after[j], x, :, c, :, high], over_x)
        pass_on(7, j, out_ref.at[after[j], x, 1 - y, c, :, high], core)

    def third(j):
        copies[4, j].wait_recv()
        pass_on(8, j, out_ref.at[after[j], :, 1 - y, c, :, low], core)
        copies[6, j].wait_recv()
        pass_on(9, j, out_ref.at[after[j], 1 - x, :, c, :, high], core)

    for j in range(slabs + 2):
        if j < slabs:
            first(j)
        if 0 <= j - 1 < slabs:
            second(j - 1)
        if 0 <= j - 2:
            third(j - 2)
    for (kind, _), copy in copies.items():
        if kind in (3, 5, 7, 8, 9):
            copy.wait_recv()
        copy.wait_send()


def gather(rows, groups):
    slabs = groups // 2
    tok, width = rows.shape
    half = width // LANES // 2 * LANES
    dma = pltpu.SemaphoreType.DMA
    out = pl.pallas_call(
        functools.partial(gather_kernel, slabs, half),
        out_shape=jax.ShapeDtypeStruct((slabs, 2, 2, 2, tok, width), rows.dtype),
        in_specs=[pl.BlockSpec(memory_space=pltpu.VMEM)],
        out_specs=pl.BlockSpec(memory_space=pltpu.VMEM),
        scratch_shapes=[dma] + [dma((slabs,))] * 20,
        compiler_params=pltpu.CompilerParams(
            collective_id=2, has_side_effects=True, vmem_limit_bytes=VMEM_LIMIT // 2
        ),
    )(rows)
    return out.reshape(slabs * 8 * tok, width)


def on_device(
    queries,
    keys,
    values,
    document_index,
    out_proj,
    residual_in,
    norm_gain,
    expert_ids,
    gate_weights,
    w_gate_up,
    w_down,
):
    groups, tensors = lax.axis_size("group"), lax.axis_size("tensor")
    experts = groups * tensors
    tok_dev, model_width = residual_in.shape
    head_out = attention(queries, keys, values, document_index)
    attended = project(head_out, out_proj, groups, tok_dev)
    hidden = residual_in.astype(jnp.float32) + attended
    mean_square = jnp.mean(hidden * hidden, axis=-1, keepdims=True)
    normed = (hidden * lax.rsqrt(mean_square + 1e-06) * norm_gain).astype(jnp.bfloat16)
    gates = jnp.sum(
        jnp.where(
            expert_ids[:, :, None] == jnp.arange(experts, dtype=jnp.int32)[None, None, :],
            gate_weights[:, :, None],
            0.0,
        ),
        axis=1,
    )
    high = lax.reduce_precision(gates, 8, 7)
    low = gates - high
    pad = -(2 * experts) % LANES
    extra = jnp.concatenate(
        [high, low, jnp.zeros((tok_dev, pad), jnp.float32)], axis=1
    ).astype(jnp.bfloat16)
    rows = jnp.concatenate([normed, extra], axis=1)
    on_chip = experts * rows.size * 2 * 4 <= VMEM_LIMIT and tensors == 4
    if on_chip:
        rows_all = gather(rows, groups)
    else:
        rows_all = lax.all_gather(rows, ("group", "tensor"), axis=0, tiled=True)
    me = lax.axis_index("group") * tensors + lax.axis_index("tensor")
    picked = jnp.arange(extra.shape[1], dtype=jnp.int32) % experts == me
    picked = picked & (jnp.arange(extra.shape[1], dtype=jnp.int32) < 2 * experts)
    gate_col = jnp.sum(
        jnp.where(picked[None, :], rows_all[:, model_width:].astype(jnp.float32), 0.0),
        axis=1,
        keepdims=True,
    )
    gate_up = w_gate_up[0]
    down_rows = w_down[0]
    ff_width = down_rows.shape[0]
    projected = jnp.dot(rows_all[:, :model_width], gate_up, preferred_element_type=jnp.float32)
    activated = (jax.nn.silu(projected[:, :ff_width]) * projected[:, ff_width:]).astype(
        jnp.bfloat16
    )
    expert_out = jnp.dot(activated, down_rows, preferred_element_type=jnp.float32)
    weighted = (expert_out * gate_col).astype(jnp.bfloat16)
    if on_chip:
        return combine(weighted, hidden, groups)
    expert_sum = lax.psum_scatter(weighted, ("group", "tensor"), scatter_dimension=0, tiled=True)
    return (hidden + expert_sum.astype(jnp.float32)).astype(jnp.bfloat16)


def solution(mesh):
    in_specs = (
        P("group", "tensor"),
        P("group", "tensor"),
        P("group", "tensor"),
        P("group", None),
        P("tensor", "group"),
        P(("group", "tensor"), None),
        P(),
        P(("group", "tensor"), None),
        P(("group", "tensor"), None),
        P(("group", "tensor"), None, None),
        P(("group", "tensor"), None, None),
    )
    out_specs = P(("group", "tensor"), None)
    return jax.shard_map(
        on_device, mesh=mesh, in_specs=in_specs, out_specs=out_specs, check_vma=False
    )
```

profile of v0, /device:TPU:0, one launch (start us, length us, event | category | flops | bytes accessed | tf_op | source)
XLA Modules:
  0.0 194.6 jit_solution(9066939460488798312)
XLA Ops:
  0.0 0.0 copy-start
  0.0 0.0 copy-start.3
  0.0 0.0 copy-start.2
  0.0 0.8 fusion.14
  0.8 0.8 copy.22
  1.6 0.8 copy.23
  2.4 0.1 select_reduce_fusion.1
  2.5 0.0 copy-done
  2.5 1.0 fusion.20
  3.5 0.1 fusion.9
  3.7 1.0 convolution_convert_fusion
  4.7 0.9 copy.27.head_ref
  5.6 54.4 %shard_map.109 = f32[32,4096]{1,0:T(8,128)} custom-call(bf16[128,1024]{1,0:T(8,128)(2,1)} %copy.27.head_ref, bf16[1024,512]{1,0:T(8,128)(2,1)} %w_ref.1), custom_call_target="tpu_custom_call" | custom-call | tf_op jit(solution)/shard_map/pallas_call | solution.py:197
  59.9 0.0 copy-done.2
  60.0 1.2 multiply_reduce_fusion
  61.2 0.0 copy-start.1
  61.2 0.0 copy-done.3
  61.2 0.1 multiply_convert_fusion.1
  61.3 0.1 concatenate.6.rows_ref
  61.4 0.0 slice-start
  61.5 52.9 %shard_map.110 = bf16[4,2,2,2,32,4224]{5,4,3,2,1,0:T(8,128)(2,1)S(1)} custom-call(bf16[32,4224]{1,0:T(8,128)(2,1)S(1)} %concatenate.6.rows_ref), custom_call_target="tpu_custom_call" | custom-call | tf_op jit(solution)/shard_map/pallas_call | solution.py:500
  114.3 0.1 select_reduce_fusion
  114.5 0.0 slice-start.1
  114.5 15.8 %fusion = f32[1024,1536]{1,0:T(8,128)S(1)} fusion(bf16[1,4096,1536]{2,1,0:T(8,128)(2,1)} %param.20, bf16[1024,4224]{1,0:T(8,128)(2,1)S(1)} %bitcast.43), kind=kOutput, calls=%fused_computation.1 | convolution fusion | flops 12884901888 | bytes 27262976 | tf_op jit(solution)/shard_map/dot_general | solution.py:565
  130.3 0.0 copy-done.1
  130.3 0.0 slice-done
  130.3 0.0 slice-done.1
  130.3 9.0 %multiply_convert_fusion = bf16[1024,4096]{1,0:T(8,128)(2,1)} fusion(f32[1024]{0:T(1024)S(1)} %select_reduce_fusion, bf16[1,768,4096]{2,1,0:T(8,128)(2,1)S(1)} %bitcast.48, f32[1024,1536]{1,0:T(8,128)S(1)} %fusion), kind=kOutput, calls=%fused_computation | convolution fusion | flops 6455558144 | bytes 20975616 | tf_op jit(solution)/shard_map/dot_general | solution.py:569
  139.3 53.6 %shard_map.111 = bf16[32,4096]{1,0:T(8,128)(2,1)} custom-call(bf16[4,2,2,2,32,4096]{5,4,3,2,1,0:T(8,128)(2,1)} %bitcast.44, f32[32,4096]{1,0:T(8,128)} %copy-done.1), custom_call_target="tpu_custom_call" | custom-call | tf_op jit(solution)/shard_map/pallas_call | solution.py:412
  192.9 1.7 copy.36
  (5 shorter events, 0.0 us)
Async XLA Ops:
  0.0 2.5 %copy-start = (bf16[128,1024]{1,0:T(8,128)(2,1)S(1)}, bf16[128,1024]{1,0:T(8,128)(2,1)}, u32[]{:S(2)}) copy-start(bf16[128,1024]{1,0:T(8,128)(2,1)} %param.11) | copy-start | bytes 786436
  0.0 61.2 %copy-start.3 = (f32[4096]{0:T(1024)S(1)}, f32[4096]{0:T(1024)}, u32[]{:S(2)}) copy-start(f32[4096]{0:T(1024)} %param.17) | copy-start | bytes 49156
  0.0 59.9 %copy-start.2 = (bf16[32,4096]{1,0:T(8,128)(2,1)S(1)}, bf16[32,4096]{1,0:T(8,128)(2,1)}, u32[]{:S(2)}) copy-start(bf16[32,4096]{1,0:T(8,128)(2,1)} %param.16) | copy-start | bytes 786436
  61.2 69.1 %copy-start.1 = (f32[32,4096]{1,0:T(8,128)}, f32[32,4096]{1,0:T(8,128)S(1)}, u32[]{:S(2)}) copy-start(f32[32,4096]{1,0:T(8,128)S(1)} %get-tuple-element.6.hidden_ref) | copy-start | bytes 1572868
  61.4 68.9 %slice-start = ((s8[6291456]{0:T(1024)(128)(4,1)}), s8[4194304]{0:T(1024)(128)(4,1)S(1)}, s32[]{:S(2)}) async-start(s8[6291456]{0:T(1024)(128)(4,1)} %bitcast.47), calls=%async_computation | async-start | bytes 8388608
  114.5 15.9 %slice-start.1 = ((s8[6291456]{0:T(1024)(128)(4,1)}), s8[2097152]{0:T(1024)(128)(4,1)S(1)}, s32[]{:S(2)}) async-start(s8[6291456]{0:T(1024)(128)(4,1)} %bitcast.47), calls=%async_computation.1 | async-start | bytes 4194304
where the time goes:
time: 195 us
  Pallas kernels  161 us (83%)
  matrix products  26.8 us (14%)
  local copies, waits for them, and re-layouts  4.17 us (2%)
  other arithmetic  2.57 us (1%)
    pallas_call x1, Pallas kernels, project(): pl.pallas_call(functools.partial(project_kernel, slabs), out_shape=jax.Sh...  54.4 us
    pallas_call x1, Pallas kernels, combine(): pl.pallas_call(functools.partial(combine_kernel, slabs), out_shape=jax.Sh...  53.6 us
    pallas_call x1, Pallas kernels, gather(): pl.pallas_call(functools.partial(gather_kernel, slabs, half), out_shape=j...  52.9 us
    dot_general x1, matrix products, on_device(): jnp.dot(rows_all[:, :model_width], gate_up, preferred_element_type=jnp.fl...  15.8 us
    dot_general x1, matrix products, on_device(): jnp.dot(activated, down_rows, preferred_element_type=jnp.float32)  8.99 us

commit v1 on v0

v1 whole, which is shorter than its diff:
```python
import functools

import jax
import jax.numpy as jnp
from jax import lax
from jax.experimental import pallas as pl
from jax.experimental.pallas import tpu as pltpu
from jax.sharding import PartitionSpec as P

HEAD_SIZE = 128
LANES = 128
MESH = pl.DeviceIdType.MESH
VMEM_LIMIT = 62 * 1024 * 1024
F32 = jnp.float32
BF16 = jnp.bfloat16


def attention(queries, keys, values, document_index):
    token_group = queries.shape[0]
    kv_dev = keys.shape[1] // HEAD_SIZE
    query_dev = queries.shape[1] // HEAD_SIZE
    group_ratio = query_dev // kv_dev
    query_head_split = queries.reshape(token_group, kv_dev, group_ratio, HEAD_SIZE)
    key_head_split = keys.reshape(token_group, kv_dev, HEAD_SIZE)
    value_head_split = values.reshape(token_group, kv_dev, HEAD_SIZE)
    scores = jnp.einsum(
        "qgrd,kgd->grqk", query_head_split, key_head_split, preferred_element_type=F32
    ) * (1.0 / HEAD_SIZE**0.5)
    doc_row = document_index[0]
    positions = jnp.arange(token_group, dtype=jnp.int32)
    visible = (positions[:, None] >= positions[None, :]) & (doc_row[:, None] == doc_row[None, :])
    scores = jnp.where(visible, scores, -jnp.inf)
    row_max = jnp.max(scores, axis=-1, keepdims=True)
    exponent = jnp.where(visible, jnp.exp(scores - row_max), 0.0)
    weights = (exponent / jnp.sum(exponent, axis=-1, keepdims=True)).astype(BF16)
    head_out = jnp.einsum("grqk,kgd->qgrd", weights, value_head_split, preferred_element_type=F32)
    return head_out.astype(BF16).reshape(token_group, query_dev * HEAD_SIZE)


def device(z, x, y, c):
    return (z * 2 + x, y * 2 + c)


def layer_kernel(
    slabs,
    copies_max,
    head_ref,
    proj_ref,
    res_ref,
    gain_ref,
    gate_ref,
    gate_up_hbm,
    down_hbm,
    out_ref,
    proj_x,
    heads,
    res_in,
    part,
    got_half,
    sum_half,
    got_y,
    gates,
    rows,
    scaled,
    squares,
    acc,
    act,
    gate_up,
    down,
    hidden,
    got_core,
    got_a,
    got_b,
    last_a,
    last_b,
    landed,
    load_sem,
    send_sems,
    recv_sems,
):
    g, t = lax.axis_index("group"), lax.axis_index("tensor")
    z, x, y, c = g // 2, g % 2, t // 2, t % 2
    tok, model = res_ref.shape
    plane = model // slabs
    width = plane // 2
    ff2 = gate_up.shape[2]
    ff = ff2 // 2
    experts = slabs * 8
    block = slabs * tok
    after = [lax.rem(z + j, slabs) for j in range(slabs)]
    before = [lax.rem(z + slabs - j, slabs) for j in range(slabs)]
    core, over_y, over_x = device(z, x, y, 1 - c), device(z, x, 1 - y, c), device(z, 1 - x, y, c)
    up = [device(before[j], x, y, c) for j in range(slabs)]
    own_cols = pl.ds(pl.multiple_of(x * width, width), width)
    other_cols = pl.ds(pl.multiple_of((1 - x) * width, width), width)

    loads = [
        pltpu.make_async_copy(
            gate_up_hbm.at[pl.ds(pl.multiple_of(after[j] * plane, plane), plane)],
            gate_up.at[j],
            load_sem.at[j],
        )
        for j in range(slabs)
    ]
    loads.append(pltpu.make_async_copy(down_hbm, down, load_sem.at[slabs]))
    for load in loads:
        load.start()

    barrier = pltpu.get_barrier_semaphore()
    partners = [core, over_y, over_x] + up[1:]
    for partner in partners:
        pl.semaphore_signal(barrier, inc=1, device_id=partner, device_id_type=MESH)
    pl.semaphore_wait(barrier, len(partners))

    count = [0]
    pending = []

    def send(src, dst, target):
        k = count[0]
        count[0] = k + 1
        copy = pltpu.make_async_remote_copy(
            src_ref=src,
            dst_ref=dst,
            send_sem=send_sems.at[k],
            recv_sem=recv_sems.at[k],
            device_id=target,
            device_id_type=MESH,
        )
        copy.start()
        pending.append(copy)
        return copy

    proj_copy = send(proj_ref, proj_x, over_x)
    head_copy = [None] + [send(head_ref, heads.at[j - 1], up[j]) for j in range(1, slabs)]
    res_copy = [None] + [
        send(
            res_ref.at[:, pl.ds(pl.multiple_of(before[j] * plane, plane), plane)],
            res_in.at[j - 1],
            up[j],
        )
        for j in range(1, slabs)
    ]
    gate_copy = [send(gate_ref, gates.at[z, x, y, c], up[j]) for j in range(1, slabs)]
    gates[z, x, y, c] = gate_ref[...]
    squares[...] = jnp.zeros_like(squares)

    def project(j, weights, columns):
        source = head_ref if j == 0 else heads.at[j - 1]
        got = jnp.dot(source[...], weights[...], preferred_element_type=F32)
        for yy in range(2):
            for cc in range(2):
                start = (yy * 2 + cc) * tok
                part[j, cc, yy, :, columns] = got[start : start + tok]

    half_copy, y_copy = {}, {}

    def over_cores(j):
        half_copy[j].wait_recv()
        total = part[j, c, 1 - y] + got_half[j, 1 - y]
        sum_half[j] = total.astype(BF16)
        y_copy[j] = send(sum_half.at[j], got_y.at[j], over_y)
        part[j, c, y] = part[j, c, y] + got_half[j, y]

    def finish(j):
        y_copy[j].wait_recv()
        if j:
            res_copy[j].wait_recv()
            residual = res_in[j - 1]
        else:
            residual = res_ref[:, pl.ds(pl.multiple_of(z * plane, plane), plane)]
        total = residual.astype(F32) + (part[j, c, y] + got_y[j].astype(F32))
        spot = pl.ds(pl.multiple_of(after[j] * tok, tok), tok)
        rows[z, x, y, c, spot, :] = total.astype(BF16)

    for j in range(slabs):
        if j:
            head_copy[j].wait_recv()
        project(j, proj_ref, own_cols)
    for copy in gate_copy:
        copy.wait_recv()
    gate_x = send(gates.at[:, x, y, c], gates.at[:, x, y, c], over_x)
    proj_copy.wait_recv()
    for j in range(slabs):
        project(j, proj_x, other_cols)
        half_copy[j] = send(part.at[j, 1 - c], got_half.at[j], core)
        if j >= 1:
            over_cores(j - 1)
    over_cores(slabs - 1)
    for j in range(slabs):
        finish(j)

    low, high = pl.ds(0, width), pl.ds(width, width)
    g_copy = {}
    g_start = len(pending)

    def pass_on(kind, j, spot, target):
        g_copy[kind, j] = send(spot, spot, target)

    for j in range(1, slabs):
        pass_on(0, j, rows.at[z, x, y, c], up[j])

    def first(j):
        if j:
            g_copy[0, j].wait_recv()
        pass_on(1, j, rows.at[after[j], x, y, c, :, low], over_x)
        pass_on(2, j, rows.at[after[j], x, y, c, :, high], over_y)
        pass_on(3, j, rows.at[after[j], x, y, c], core)

    def second(j):
        g_copy[1, j].wait_recv()
        pass_on(4, j, rows.at[after[j], :, y, c, :, low], over_y)
        pass_on(5, j, rows.at[after[j], 1 - x, y, c, :, low], core)
        g_copy[2, j].wait_recv()
        pass_on(6, j, rows.at[after[j], x, :, c, :, high], over_x)
        pass_on(7, j, rows.at[after[j], x, 1 - y, c, :, high], core)

    def third(j):
        g_copy[4, j].wait_recv()
        pass_on(8, j, rows.at[after[j], :, 1 - y, c, :, low], core)
        g_copy[6, j].wait_recv()
        pass_on(9, j, rows.at[after[j], 1 - x, :, c, :, high], core)

    def up_project(j):
        for kind in (3, 5, 7, 8, 9):
            g_copy[kind, j].wait_recv()
        p = after[j]
        gain_cols = pl.ds(pl.multiple_of(p * plane, plane), plane)

        @pl.loop(0, 8)
        def _(b):
            @pl.loop(0, slabs)
            def _(s):
                spot = pl.ds(pl.multiple_of(s * tok, tok), tok)
                value = rows[p, b // 4, (b // 2) % 2, b % 2, spot, :].astype(F32)
                place = pl.ds(pl.multiple_of(b * block + s * tok, tok), tok)
                square = squares[place, :]
                for lane in range(plane // LANES):
                    piece = value[:, lane * LANES : (lane + 1) * LANES]
                    square = square + piece * piece
                squares[place, :] = square
                scaled[place, :] = (value * gain_ref[:, gain_cols]).astype(BF16)

        loads[j].wait()
        step = 512

        @pl.loop(0, ff2 // step)
        def _(n):
            columns = pl.ds(pl.multiple_of(n * step, step), step)
            got = jnp.dot(
                scaled[...], gate_up[j, :, columns], preferred_element_type=F32
            )
            if j:
                acc[:, columns] = acc[:, columns] + got
            else:
                acc[:, columns] = got

    first(0)
    gate_x.wait_recv()
    gate_y = send(gates.at[:, :, y, c], gates.at[:, :, y, c], over_y)
    second(0)
    if slabs > 1:
        first(1)
    third(0)
    gate_y.wait_recv()
    gate_c = send(gates.at[:, :, :, c], gates.at[:, :, :, c], core)
    for j in range(slabs):
        if j + 1 < slabs:
            second(j + 1)
        if j + 2 < slabs:
            first(j + 2)
        up_project(j)
        if j + 1 < slabs:
            third(j + 1)
    gate_c.wait_recv()
    own = pl.ds(pl.multiple_of(z * tok, tok), tok)
    for q in range(slabs):
        hidden[q] = rows[q, x, y, c, own, :]
    for copy in pending[g_start:]:
        copy.wait_send()
    g_end = len(pending)
    loads[slabs].wait()

    me = g * 4 + t
    lane = lax.broadcasted_iota(jnp.int32, (tok, LANES), 1)
    picked = (lane == me) | (lane == me + experts)
    halves = slabs // 2
    quarters = [pl.ds(0, halves), pl.ds(halves, slabs - halves)]

    def spots(j):
        return pl.ds(j * tok, tok)

    c_copy, a_copy, b_copy, la_copy, lb_copy, z_copy = {}, {}, {}, {}, {}, {}

    def down_project(j):
        p = after[j]
        for cc in range(2):
            for xx in range(2):
                for yy in range(2):
                    source = c if cc == 0 else 1 - c
                    b = xx * 4 + yy * 2 + source
                    place = pl.ds(pl.multiple_of(b * block + p * tok, tok), tok)
                    mean = jnp.sum(squares[place, :], axis=-1, keepdims=True) * (1.0 / model)
                    scale = lax.rsqrt(mean + 1e-06)
                    gate = jnp.sum(
                        jnp.where(picked, gates[p, xx, yy, source].astype(F32), 0.0),
                        axis=-1,
                        keepdims=True,
                    )
                    left = acc[place, :ff] * scale
                    right = acc[place, ff:] * (scale * gate)
                    value = left / (1.0 + jnp.exp(-left)) * right
                    spot = ((cc * 2 + xx) * 2 + yy) * tok
                    act[spot : spot + tok, :] = value.astype(BF16)
        step = plane // 2

        @pl.loop(0, model // step)
        def _(n):
            got = jnp.dot(
                act[...],
                down[:, pl.ds(pl.multiple_of(n * step, step), step)],
                preferred_element_type=F32,
            ).astype(BF16)
            columns = pl.ds(pl.multiple_of((n % 2) * step, step), step)
            for cc in range(2):
                for xx in range(2):
                    for yy in range(2):
                        spot = ((cc * 2 + xx) * 2 + yy) * tok
                        rows[n // 2, xx, yy, 1 - cc, spots(j), columns] = got[spot : spot + tok]

        c_copy[j] = [
            send(rows.at[q, :, :, 0, spots(j)], got_core.at[j, q], core) for q in quarters
        ]

    def add_cores(j):
        for h in range(2):
            c_copy[j][h].wait_recv()

            @pl.loop(quarters[h].start, quarters[h].start + quarters[h].size)
            def _(q):
                for xx in range(2):
                    for yy in range(2):
                        total = rows[q, xx, yy, 1, spots(j), :].astype(F32) + got_core[
                            j, q, xx, yy
                        ].astype(F32)
                        rows[q, xx, yy, 1, spots(j), :] = total.astype(BF16)

            if h == 0:
                a_copy[j] = send(
                    rows.at[quarters[0], 1 - x, :, 1, spots(j)], got_a.at[j], over_x
                )
            else:
                b_copy[j] = send(
                    rows.at[quarters[1], :, 1 - y, 1, spots(j)], got_b.at[j], over_y
                )

    def add_second(j):
        a_copy[j].wait_recv()
        for q in range(halves):
            for yy in range(2):
                total = rows[q, x, yy, 1, spots(j), :].astype(F32) + got_a[j, q, yy].astype(F32)
                rows[q, x, yy, 1, spots(j), :] = total.astype(BF16)
        la_copy[j] = send(rows.at[quarters[0], x, 1 - y, 1, spots(j)], last_a.at[j], over_y)
        b_copy[j].wait_recv()
        for q in range(slabs - halves):
            for xx in range(2):
                total = rows[halves + q, xx, y, 1, spots(j), :].astype(F32) + got_b[
                    j, q, xx
                ].astype(F32)
                rows[halves + q, xx, y, 1, spots(j), :] = total.astype(BF16)
        lb_copy[j] = send(rows.at[quarters[1], 1 - x, y, 1, spots(j)], last_b.at[j], over_x)

    def add_third(j):
        la_copy[j].wait_recv()
        lb_copy[j].wait_recv()
        for q in range(slabs):
            last = last_a[j, q] if q < halves else last_b[j, q - halves]
            total = rows[q, x, y, 1, spots(j), :].astype(F32) + last.astype(F32)
            rows[q, x, y, 1, spots(j), :] = total.astype(BF16)
        if j:
            z_copy[j] = send(
                rows.at[:, x, y, 1, spots(j)], landed.at[j - 1], device(after[j], x, y, c)
            )

    order = list(range(1, slabs)) + [0]
    for i, j in enumerate(order):
        down_project(j)
        if i >= 1:
            add_cores(order[i - 1])
        if i >= 2:
            add_second(order[i - 2])
        if i >= 3:
            add_third(order[i - 3])
    add_cores(order[-1])
    for j in order[max(slabs - 2, 0) :]:
        add_second(j)
        if j == order[-1]:
            break
        if slabs >= 3:
            add_third(order[order.index(j) - 1])
    for j in order[max(slabs - 2, 0) :]:
        add_third(j)
    for j in range(1, slabs):
        z_copy[j].wait_recv()
    for q in range(slabs):
        total = hidden[q].astype(F32) + rows[q, x, y, 1, spots(0), :].astype(F32)
        for j in range(1, slabs):
            total = total + landed[j - 1, q].astype(F32)
        out_ref[:, q * plane : (q + 1) * plane] = total.astype(BF16)
    for copy in pending[:g_start] + pending[g_end:]:
        copy.wait_send()
    assert count[0] <= copies_max, count[0]


def layer(head_out, out_proj, residual, gain, gates, gate_up, down, groups):
    slabs = groups // 2
    tok, model = residual.shape
    tokens, depth = head_out.shape
    plane = model // slabs
    ff, ff2 = down.shape[0], gate_up.shape[1]
    total = tok * slabs * 8
    halves = slabs // 2
    copies_max = 128
    dma = pltpu.SemaphoreType.DMA
    vmem = pl.BlockSpec(memory_space=pltpu.VMEM)
    hbm = pl.BlockSpec(memory_space=pl.ANY)
    return pl.pallas_call(
        functools.partial(layer_kernel, slabs, copies_max),
        out_shape=jax.ShapeDtypeStruct((tok, model), BF16),
        in_specs=[vmem] * 5 + [hbm] * 2,
        out_specs=vmem,
        scratch_shapes=[
            pltpu.VMEM(out_proj.shape, BF16),
            pltpu.VMEM((slabs - 1, tokens, depth), BF16),
            pltpu.VMEM((slabs - 1, tok, plane), BF16),
            pltpu.VMEM((slabs, 2, 2, tok, plane), F32),
            pltpu.VMEM((slabs, 2, tok, plane), F32),
            pltpu.VMEM((slabs, tok, plane), BF16),
            pltpu.VMEM((slabs, tok, plane), BF16),
            pltpu.VMEM((slabs, 2, 2, 2, tok, LANES), BF16),
            pltpu.VMEM((slabs, 2, 2, 2, slabs * tok, plane), BF16),
            pltpu.VMEM((total, plane), BF16),
            pltpu.VMEM((total, LANES), F32),
            pltpu.VMEM((total, ff2), F32),
            pltpu.VMEM((8 * tok, ff), BF16),
            pltpu.VMEM((slabs, plane, ff2), BF16),
            pltpu.VMEM((ff, model), BF16),
            pltpu.VMEM((slabs, tok, plane), BF16),
            pltpu.VMEM((slabs, slabs, 2, 2, tok, plane), BF16),
            pltpu.VMEM((slabs, halves, 2, tok, plane), BF16),
            pltpu.VMEM((slabs, slabs - halves, 2, tok, plane), BF16),
            pltpu.VMEM((slabs, halves, tok, plane), BF16),
            pltpu.VMEM((slabs, slabs - halves, tok, plane), BF16),
            pltpu.VMEM((slabs - 1, slabs, tok, plane), BF16),
            dma((slabs + 1,)),
            dma((copies_max,)),
            dma((copies_max,)),
        ],
        compiler_params=pltpu.CompilerParams(
            collective_id=0, has_side_effects=True, vmem_limit_bytes=VMEM_LIMIT
        ),
    )(head_out, out_proj, residual, gain, gates, gate_up, down)


def spread_gates(expert_ids, gate_weights, experts):
    gates = jnp.sum(
        jnp.where(
            expert_ids[:, :, None] == jnp.arange(experts, dtype=jnp.int32)[None, None, :],
            gate_weights[:, :, None],
            0.0,
        ),
        axis=1,
    )
    high = lax.reduce_precision(gates, 8, 7)
    low = gates - high
    pad = -(2 * experts) % LANES
    return jnp.concatenate(
        [high, low, jnp.zeros((gates.shape[0], pad), F32)], axis=1
    ).astype(BF16)


def plain_layer(head_out, out_proj, residual, gain, extra, gate_up, down, groups, tensors):
    experts = groups * tensors
    tok, model = residual.shape
    heads = lax.all_gather(head_out, "group", axis=0, tiled=True)
    part = jnp.dot(heads, out_proj, preferred_element_type=F32)
    part = part.reshape(groups, tensors, tok, part.shape[1])
    part = lax.psum_scatter(part, "tensor", scatter_dimension=1, tiled=False)
    attended = lax.all_to_all(part, "group", split_axis=0, concat_axis=2, tiled=True)
    hidden = residual.astype(F32) + attended.reshape(tok, model)
    mean_square = jnp.mean(hidden * hidden, axis=-1, keepdims=True)
    normed = (hidden * lax.rsqrt(mean_square + 1e-06) * gain).astype(BF16)
    rows = jnp.concatenate([normed, extra], axis=1)
    rows_all = lax.all_gather(rows, ("group", "tensor"), axis=0, tiled=True)
    me = lax.axis_index("group") * tensors + lax.axis_index("tensor")
    lane = jnp.arange(extra.shape[1], dtype=jnp.int32)
    picked = (lane == me) | (lane == me + experts)
    gate_col = jnp.sum(
        jnp.where(picked[None, :], rows_all[:, model:].astype(F32), 0.0), axis=1, keepdims=True
    )
    ff = down.shape[0]
    projected = jnp.dot(rows_all[:, :model], gate_up, preferred_element_type=F32)
    activated = (jax.nn.silu(projected[:, :ff]) * projected[:, ff:]).astype(BF16)
    expert_out = jnp.dot(activated, down, preferred_element_type=F32)
    weighted = (expert_out * gate_col).astype(BF16)
    expert_sum = lax.psum_scatter(weighted, ("group", "tensor"), scatter_dimension=0, tiled=True)
    return (hidden + expert_sum.astype(F32)).astype(BF16)


def on_device(
    queries,
    keys,
    values,
    document_index,
    out_proj,
    residual_in,
    norm_gain,
    expert_ids,
    gate_weights,
    w_gate_up,
    w_down,
):
    groups, tensors = lax.axis_size("group"), lax.axis_size("tensor")
    experts = groups * tensors
    gain = norm_gain[None, :]
    head_out = attention(queries, keys, values, document_index)
    extra = spread_gates(expert_ids, gate_weights, experts)
    if groups == 8 and tensors == 4:
        return layer(
            head_out, out_proj, residual_in, gain, extra, w_gate_up[0], w_down[0], groups
        )
    return plain_layer(
        head_out, out_proj, residual_in, gain, extra, w_gate_up[0], w_down[0], groups, tensors
    )


def solution(mesh):
    in_specs = (
        P("group", "tensor"),
        P("group", "tensor"),
        P("group", "tensor"),
        P("group", None),
        P("tensor", "group"),
        P(("group", "tensor"), None),
        P(),
        P(("group", "tensor"), None),
        P(("group", "tensor"), None),
        P(("group", "tensor"), None, None),
        P(("group", "tensor"), None, None),
    )
    out_specs = P(("group", "tensor"), None)
    return jax.shard_map(
        on_device, mesh=mesh, in_specs=in_specs, out_specs=out_specs, check_vma=False
    )
```

time: 195 us -> 155 us (0.79)
  matrix products: 26.8 us -> 2.03 us
  Pallas kernels: 161 us -> 146 us
    dot_general x2 -> x0, matrix products: 24.8 us -> none  [the longest x1 15.8 us: on_device(): jnp.dot(rows_all[:, :model_width], gate_up, preferred_element_type=jnp.fl...]
    pallas_call x3 -> x1, Pallas kernels: 161 us -> 146 us  [layer(): pl.pallas_call(functools.partial(layer_kernel, slabs, copies_max), out_sh...]
where the time goes in v1:
time: 155 us
  Pallas kernels  146 us (94%)
  local copies, waits for them, and re-layouts  4.28 us (3%)
  matrix products  2.03 us (1%)
  other arithmetic  1.74 us (1%)
    pallas_call x1, Pallas kernels, layer(): pl.pallas_call(functools.partial(layer_kernel, slabs, copies_max), out_sh...  146 us
    unnamed x5, local copies, waits for them, and re-layouts  3.35 us

profile of v1, /device:TPU:0, one launch (start us, length us, event | category | flops | bytes accessed | tf_op | source)
XLA Modules:
  0.0 154.5 jit_solution(11711236508455430667)
XLA Ops:
  0.0 0.0 copy-start
  0.0 0.8 fusion.7
  0.8 0.2 copy-done
  1.0 1.0 fusion.12
  2.0 0.1 fusion.2
  2.1 1.0 convolution_convert_fusion
  3.1 0.9 copy.27.head_ref
  4.0 0.8 copy.22
  4.8 0.8 copy.23
  5.5 0.1 select_reduce_fusion
  5.7 0.1 pad.2.clone
  5.8 0.7 maximum_maximum_fusion.gate_ref
  6.4 146.4 %shard_map.109 = bf16[32,4096]{1,0:T(8,128)(2,1)} custom-call(bf16[128,1024]{1,0:T(8,128)(2,1)} %copy.27.head_ref, bf16[1024,512]{1,0:T(8,128)(2,1)} %proj_ref.1, bf16[32,4096]{1,0:T(8,128)(2,1)} %res_ref.1, f32[1,4096]{1,0:T(1,128)} %bitcast.40, bf16[32,128]{1,0:T(8,128)(2,1)} %maximum_maximum_fusion.gate_ref, bf16[4096,1536]{1,0:T(8,128)(2,1)} %bitcast.37, ...), custom_call_target="tpu_custom_call" | custom-call | tf_op jit(solution)/shard_map/pallas_call | solution.py:426
  152.9 1.7 %copy.36 = bf16[32,4096]{1,0:T(8,128)(2,1)} copy(bf16[32,4096]{1,0:T(8,128)(2,1)} %shard_map.109) | data formatting | bytes 524288
  (2 shorter events, 0.0 us)
Async XLA Ops:
  0.0 1.0 copy-start

commit v2 on v1

v2 whole, which is shorter than its diff:
```python
import functools

import jax
import jax.numpy as jnp
from jax import lax
from jax.experimental import pallas as pl
from jax.experimental.pallas import tpu as pltpu
from jax.sharding import PartitionSpec as P

HEAD_SIZE = 128
LANES = 128
MESH = pl.DeviceIdType.MESH
VMEM_LIMIT = 62 * 1024 * 1024
F32 = jnp.float32
BF16 = jnp.bfloat16


def attention(queries, keys, values, document_index):
    token_group = queries.shape[0]
    kv_dev = keys.shape[1] // HEAD_SIZE
    query_dev = queries.shape[1] // HEAD_SIZE
    group_ratio = query_dev // kv_dev
    query_head_split = queries.reshape(token_group, kv_dev, group_ratio, HEAD_SIZE)
    key_head_split = keys.reshape(token_group, kv_dev, HEAD_SIZE)
    value_head_split = values.reshape(token_group, kv_dev, HEAD_SIZE)
    scores = jnp.einsum(
        "qgrd,kgd->grqk", query_head_split, key_head_split, preferred_element_type=F32
    ) * (1.0 / HEAD_SIZE**0.5)
    doc_row = document_index[0]
    positions = jnp.arange(token_group, dtype=jnp.int32)
    visible = (positions[:, None] >= positions[None, :]) & (doc_row[:, None] == doc_row[None, :])
    scores = jnp.where(visible, scores, -jnp.inf)
    row_max = jnp.max(scores, axis=-1, keepdims=True)
    exponent = jnp.where(visible, jnp.exp(scores - row_max), 0.0)
    weights = (exponent / jnp.sum(exponent, axis=-1, keepdims=True)).astype(BF16)
    head_out = jnp.einsum("grqk,kgd->qgrd", weights, value_head_split, preferred_element_type=F32)
    return head_out.astype(BF16).reshape(token_group, query_dev * HEAD_SIZE)


def device(z, x, y, c):
    return (z * 2 + x, y * 2 + c)


def nearest_first(z):
    first = jnp.where(z == 0, 1, jnp.where(z == 1, 2, jnp.where(z == 2, 1, 2)))
    second = jnp.where(z == 0, 2, jnp.where(z == 1, 0, jnp.where(z == 2, 3, 1)))
    third = jnp.where(z <= 1, 3, 0)
    return [first, second, third]


def layer_kernel(
    slabs,
    copies_max,
    query_hbm,
    key_hbm,
    value_hbm,
    doc_ref,
    proj_hbm,
    res_hbm,
    gain_ref,
    ids_ref,
    weight_ref,
    gate_up_hbm,
    down_hbm,
    out_ref,
    query_ref,
    key_ref,
    value_ref,
    proj_ref,
    res_ref,
    head_own,
    proj_x,
    heads,
    res_in,
    part,
    got_half,
    sum_half,
    got_y,
    gates,
    rows,
    scaled,
    squares,
    acc,
    act,
    gate_up,
    down,
    hidden,
    got_core,
    got_x,
    got_y2,
    last_d,
    last_a,
    landed_a,
    landed_d,
    load_sem,
    send_sems,
    recv_sems,
):
    g, t = lax.axis_index("group"), lax.axis_index("tensor")
    z, x, y, c = g // 2, g % 2, t // 2, t % 2
    tok, model = res_ref.shape
    plane = model // slabs
    width = plane // 2
    ff2 = gate_up.shape[2]
    ff = ff2 // 2
    experts = slabs * 8
    block = slabs * tok
    others = nearest_first(z)
    planes = [z] + others
    core, over_y, over_x = device(z, x, y, 1 - c), device(z, x, 1 - y, c), device(z, 1 - x, y, c)

    def plane_cols(p):
        return pl.ds(pl.multiple_of(p * plane, plane), plane)

    small = [
        pltpu.make_async_copy(source, target, load_sem.at[slabs + 1 + i])
        for i, (source, target) in enumerate(
            [
                (key_hbm, key_ref),
                (query_hbm, query_ref),
                (value_hbm, value_ref),
                (proj_hbm, proj_ref),
                (res_hbm, res_ref),
            ]
        )
    ]
    for load in small:
        load.start()
    barrier = pltpu.get_barrier_semaphore()
    partners = [core, over_y, over_x] + [device(p, x, y, c) for p in others]
    for partner in partners:
        pl.semaphore_signal(barrier, inc=1, device_id=partner, device_id_type=MESH)
    loads = [
        pltpu.make_async_copy(
            gate_up_hbm.at[pl.ds(pl.multiple_of(planes[k] * plane, plane), plane)],
            gate_up.at[k],
            load_sem.at[k],
        )
        for k in range(slabs)
    ]
    loads.append(pltpu.make_async_copy(down_hbm, down, load_sem.at[slabs]))

    lane = lax.broadcasted_iota(jnp.int32, (tok, LANES), 1)
    gate = jnp.zeros((tok, LANES), F32)
    for k in range(ids_ref.shape[1]):
        chosen = ids_ref[:, k : k + 1]
        hit = (lane == chosen) | (lane == chosen + experts)
        gate = gate + jnp.where(hit, weight_ref[:, k : k + 1], 0.0)
    gate_high = gate.astype(BF16).astype(F32)
    gates[z, x, y, c] = jnp.where(lane < experts, gate_high, gate - gate_high).astype(BF16)
    squares[...] = jnp.zeros_like(squares)

    for load in small[:3]:
        load.wait()

    def attend():
        tokens = query_ref.shape[0]
        doc = jnp.broadcast_to(doc_ref[...].astype(F32), (tokens, tokens))
        row = lax.broadcasted_iota(jnp.int32, (tokens, tokens), 0)
        column = lax.broadcasted_iota(jnp.int32, (tokens, tokens), 1)
        visible = (row >= column) & (doc == doc.T)
        for h in range(query_ref.shape[1] // HEAD_SIZE):
            span = slice(h * HEAD_SIZE, (h + 1) * HEAD_SIZE)
            scores = lax.dot_general(
                query_ref[:, span],
                key_ref[...],
                (((1,), (1,)), ((), ())),
                preferred_element_type=F32,
            ) * (1.0 / HEAD_SIZE**0.5)
            scores = jnp.where(visible, scores, -jnp.inf)
            exponent = jnp.exp(scores - jnp.max(scores, axis=-1, keepdims=True))
            total = jnp.sum(exponent, axis=-1, keepdims=True)
            probs = (exponent / total).astype(BF16)
            head_own[:, span] = jnp.dot(
                probs, value_ref[...], preferred_element_type=F32
            ).astype(BF16)

    attend()
    for load in small[3:]:
        load.wait()
    pl.semaphore_wait(barrier, len(partners))
    for load in loads:
        load.start()

    count = [0]
    pending = []

    def copy_of(src, dst, send_index, recv_index, target):
        return pltpu.make_async_remote_copy(
            src_ref=src,
            dst_ref=dst,
            send_sem=send_sems.at[send_index],
            recv_sem=recv_sems.at[recv_index],
            device_id=target,
            device_id_type=MESH,
        )

    def take(n):
        k = count[0]
        count[0] = k + n
        return k

    def send(src, dst, target):
        k = take(1)
        copy = copy_of(src, dst, k, k, target)
        copy.start()
        pending.append(copy)
        return copy

    def send_planes(source, target):
        k = take(slabs)
        for i, p in enumerate(others):
            copy = copy_of(source(p), target(z), k + i, k + z, device(p, x, y, c))
            copy.start()
            pending.append(copy)
        return lambda p: copy_of(target(p), target(p), k, k + p, core)

    pieces = 2
    piece = width // pieces
    proj_copy = []
    for i in range(pieces):
        cols = pl.ds(i * piece, piece)
        proj_copy.append(send(proj_ref.at[:, cols], proj_x.at[:, cols], over_x))
    above = device(jnp.minimum(z + 1, slabs - 1), x, y, c)
    below = device(jnp.maximum(z - 1, 0), x, y, c)
    is_low, is_high = z < slabs - 1, z > 0
    chunks = 2
    chunk = head_own.shape[1] // chunks
    chain = [take(slabs + 2) for _ in range(chunks)]
    spans = [pl.ds(i * chunk, chunk) for i in range(chunks)]

    def own_copy(i, rising):
        return copy_of(
            head_own.at[:, spans[i]],
            heads.at[z, :, spans[i]],
            chain[i] + slabs + (0 if rising else 1),
            chain[i] + z,
            above if rising else below,
        )

    def relay_copy(i, p, target):
        spot = heads.at[p, :, spans[i]]
        return copy_of(spot, spot, chain[i] + p, chain[i] + p, target)

    def chain_do(i, p, act_on):
        if p is None:
            rising, falling = is_low, is_high
        else:
            rising, falling = (p < z) & is_low, (p > z) & is_high

        @pl.when(rising)
        def _():
            act_on(own_copy(i, True) if p is None else relay_copy(i, p, above))

        @pl.when(falling)
        def _():
            act_on(own_copy(i, False) if p is None else relay_copy(i, p, below))

    for i in range(chunks):
        chain_do(i, None, lambda copy: copy.start())

    def relay(p):
        for i in range(chunks):
            relay_copy(i, p, above).wait_recv()
            chain_do(i, p, lambda copy: copy.start())

    def project(k, weights, columns):
        source = head_own[...] if k == 0 else heads[planes[k]]
        got = jnp.dot(source, weights, preferred_element_type=F32)
        for yy in range(2):
            for cc in range(2):
                start = (yy * 2 + cc) * tok
                part[k, cc, yy, :, columns] = got[start : start + tok]

    def columns_of(i):
        if i == 0:
            return pl.ds(pl.multiple_of(x * width, width), width)
        return pl.ds(pl.multiple_of((1 - x) * width + (i - 1) * piece, piece), piece)

    half_copy, y_copy = {}, {}

    def to_core(i, ks):
        columns = columns_of(i)
        half_copy[i, ks] = send(
            part.at[pl.ds(ks[0], len(ks)), 1 - c, :, :, columns],
            got_half.at[pl.ds(ks[0], len(ks)), :, :, columns],
            core,
        )

    def over_cores(i, ks):
        columns = columns_of(i)
        half_copy[i, ks].wait_recv()
        for k in ks:
            total = part[k, c, 1 - y, :, columns] + got_half[k, 1 - y, :, columns]
            sum_half[k, :, columns] = total.astype(BF16)
        spot = pl.ds(ks[0], len(ks))
        y_copy[i, ks] = send(
            sum_half.at[spot, :, columns], got_y.at[spot, :, columns], over_y
        )
        for k in ks:
            part[k, c, y, :, columns] = part[k, c, y, :, columns] + got_half[k, y, :, columns]

    half_tok = tok // 2

    def finish(i, ks):
        columns = columns_of(i)
        y_copy[i, ks].wait_recv()
        for k in ks:
            total = part[k, c, y, :, columns] + got_y[k, :, columns].astype(F32)
            total = (total + res_in[planes[k], :, columns].astype(F32)).astype(BF16)
            spot = pl.ds(pl.multiple_of(planes[k] * half_tok, half_tok), half_tok)
            for h in range(2):
                rows[z, x, y, c, h, spot, columns] = total[h * half_tok : (h + 1) * half_tok]

    every = tuple(range(slabs))
    project(0, proj_ref[...], columns_of(0))
    to_core(0, (0,))
    for k in range(1, slabs):
        relay(planes[k])
        project(k, proj_ref[...], columns_of(0))
        to_core(0, (k,))
    res_wait = send_planes(lambda p: res_ref.at[:, plane_cols(p)], lambda p: res_in.at[p])
    gate_wait = send_planes(lambda p: gates.at[z, x, y, c], lambda p: gates.at[p, x, y, c])
    for k in range(slabs):
        over_cores(0, (k,))
    for i in range(pieces):
        proj_copy[i].wait_recv()
        for k in range(slabs):
            project(k, proj_x[:, i * piece : (i + 1) * piece], columns_of(1 + i))
        to_core(1 + i, every)
        if i == 0:
            res_in[z] = res_ref[:, plane_cols(z)]
        over_cores(1 + i, every)
    for p in others:
        res_wait(p).wait_recv()
    for k in range(slabs):
        finish(0, (k,))
    for i in range(pieces):
        finish(1 + i, every)

    low, high = pl.ds(0, width), pl.ds(width, width)
    g_copy = {}
    g_start = len(pending)
    g_marks = {}

    def pass_on(kind, unit, spot, target):
        g_copy[kind, unit] = send(spot, spot, target)

    z_wait = [
        send_planes(
            lambda p, h=h: rows.at[z, x, y, c, h], lambda p, h=h: rows.at[p, x, y, c, h]
        )
        for h in range(2)
    ]
    for p in others:
        gate_wait(p).wait_recv()
    gate_x = send(gates.at[:, x, y, c], gates.at[:, x, y, c], over_x)

    def first(h, k):
        p = planes[k]
        if k:
            z_wait[h](p).wait_recv()
        pass_on("x", (h, k), rows.at[p, x, y, c, h, :, low], over_x)
        pass_on("y", (h, k), rows.at[p, x, y, c, h, :, high], over_y)
        pass_on("c", (h, k), rows.at[p, x, y, c, h], core)

    def second(h, k):
        p = planes[k]
        g_copy["x", (h, k)].wait_recv()
        pass_on("xy", (h, k), rows.at[p, :, y, c, h, :, low], over_y)
        pass_on("xc", (h, k), rows.at[p, 1 - x, y, c, h, :, low], core)
        g_copy["y", (h, k)].wait_recv()
        pass_on("yx", (h, k), rows.at[p, x, :, c, h, :, high], over_x)
        pass_on("yc", (h, k), rows.at[p, x, 1 - y, c, h, :, high], core)

    def third(h, k):
        p = planes[k]
        g_copy["xy", (h, k)].wait_recv()
        pass_on("xyc", (h, k), rows.at[p, :, 1 - y, c, h, :, low], core)
        g_copy["yx", (h, k)].wait_recv()
        pass_on("yxc", (h, k), rows.at[p, 1 - x, :, c, h, :, high], core)

    step = 512
    half_rows = 8 * slabs * half_tok

    def up_project(h, k):
        for kind in ("c", "xc", "yc", "xyc", "yxc"):
            g_copy[kind, (h, k)].wait_recv()
        p = planes[k]
        gain_cols = plane_cols(p)
        per = block // 2 // tok

        @pl.loop(0, 8)
        def _(b):
            @pl.loop(0, per)
            def _(s):
                spot = pl.ds(pl.multiple_of(s * tok, tok), tok)
                value = rows[p, b // 4, (b // 2) % 2, b % 2, h, spot, :].astype(F32)
                place = pl.ds(pl.multiple_of((b * per + s) * tok, tok), tok)
                square = squares[h, place, :]
                for i in range(plane // LANES):
                    strip = value[:, i * LANES : (i + 1) * LANES]
                    square = square + strip * strip
                squares[h, place, :] = square
                scaled[place, :] = (value * gain_ref[:, gain_cols]).astype(BF16)

        if h == 0:
            loads[k].wait()

        @pl.loop(0, ff2 // step)
        def _(n):
            columns = pl.ds(pl.multiple_of(n * step, step), step)
            got = jnp.dot(scaled[...], gate_up[k, :, columns], preferred_element_type=F32)
            if k:
                acc[h, :, columns] = acc[h, :, columns] + got
            else:
                acc[h, :, columns] = got

    me = g * 4 + t
    half_lane = lax.broadcasted_iota(jnp.int32, (half_tok, LANES), 1)
    picked = (half_lane == me) | (half_lane == me + experts)
    halves = slabs // 2
    quarters = [pl.ds(0, halves), pl.ds(halves, slabs - halves)]
    pair = [(2, 3), (0, 1)]

    def clear(h):
        own = pl.ds(pl.multiple_of(z * half_tok, half_tok), half_tok)
        for q in range(slabs):
            hidden[q, h * half_tok : (h + 1) * half_tok] = rows[q, x, y, c, h, own, :]
        for (kind, unit), copy in g_copy.items():
            if unit[0] == h:
                copy.wait_send()
        for copy in pending[g_start + h * (slabs - 1) : g_start + (h + 1) * (slabs - 1)]:
            copy.wait_send()

    def spots(k):
        return pl.ds(k * half_tok, half_tok)

    def both(u):
        return pl.ds(pair[u][0] * half_tok, 2 * half_tok)

    cut = 3 * plane // 8 // LANES * LANES
    part_a, part_d = pl.ds(0, cut), pl.ds(cut, plane - cut)
    c_copy, x_copy, y2_copy, d_copy = {}, {}, {}, {}
    zk = [take(2 * slabs) for _ in range(2)]

    def down_project(h, u):
        for cc in range(2):
            for i, k in enumerate(pair[u]):
                p = planes[k]
                for xx in range(2):
                    for yy in range(2):
                        source = c if cc == 0 else 1 - c
                        b = xx * 4 + yy * 2 + source
                        place = pl.ds(
                            pl.multiple_of((b * slabs + p) * half_tok, half_tok), half_tok
                        )
                        mean = jnp.sum(squares[h, place, :], axis=-1, keepdims=True)
                        scale = lax.rsqrt(mean * (1.0 / model) + 1e-06)
                        mine = gates[p, xx, yy, source, h * half_tok : (h + 1) * half_tok]
                        share = jnp.sum(
                            jnp.where(picked, mine.astype(F32), 0.0), axis=-1, keepdims=True
                        )
                        left = acc[h, place, :ff] * scale
                        right = acc[h, place, ff:] * (scale * share)
                        value = left / (1.0 + jnp.exp(-left)) * right
                        spot = (((cc * 2 + xx) * 2 + yy) * 2 + i) * half_tok
                        act[spot : spot + half_tok, :] = value.astype(BF16)
        if u == 0 and h == 0:
            loads[slabs].wait()
        tile = plane // 2
        for part_of in range(2):

            @pl.loop(part_of * slabs, (part_of + 1) * slabs)
            def _(n):
                got = jnp.dot(
                    act[...],
                    down[:, pl.ds(pl.multiple_of(n * tile, tile), tile)],
                    preferred_element_type=F32,
                ).astype(BF16)
                columns = pl.ds(pl.multiple_of((n % 2) * tile, tile), tile)
                for cc in range(2):
                    for xx in range(2):
                        for yy in range(2):
                            spot = ((cc * 2 + xx) * 2 + yy) * tok
                            rows[n // 2, xx, yy, 1 - cc, h, both(u), columns] = got[
                                spot : spot + tok
                            ]

            q = quarters[part_of]
            c_copy[h, u, part_of] = send(
                rows.at[q, :, :, 0, h, both(u)], got_core.at[q, :, :, h, both(u)], core
            )

    def add_into(ref, other):
        ref[...] = (ref[...].astype(F32) + other.astype(F32)).astype(BF16)

    def add_cores(h, u):
        for part_of in range(2):
            c_copy[h, u, part_of].wait_recv()
            q0 = quarters[part_of].start

            @pl.loop(q0, q0 + quarters[part_of].size)
            def _(q):
                for xx in range(2):
                    for yy in range(2):
                        add_into(
                            rows.at[q, xx, yy, 1, h, both(u)], got_core[q, xx, yy, h, both(u)]
                        )

            q = quarters[part_of]
            x_copy[h, u, part_of] = send(
                rows.at[q, 1 - x, :, 1, h, both(u), part_d], got_x.at[q, :, h, both(u)], over_x
            )
            y2_copy[h, u, part_of] = send(
                rows.at[q, :, 1 - y, 1, h, both(u), part_a], got_y2.at[q, :, h, both(u)], over_y
            )

    def send_home(h, k, src, landing, index):
        copy = copy_of(
            src, landing.at[z, h], zk[h] + index + k, zk[h] + index + z, device(planes[k], x, y, c)
        )
        copy.start()
        pending.append(copy)

    def add_second(h, u):
        for part_of in range(2):
            q0 = quarters[part_of].start
            x_copy[h, u, part_of].wait_recv()

            @pl.loop(q0, q0 + quarters[part_of].size)
            def _(q):
                for yy in range(2):
                    add_into(rows.at[q, x, yy, 1, h, both(u), part_d], got_x[q, yy, h, both(u)])

        d_copy[h, u] = send(
            rows.at[:, x, 1 - y, 1, h, both(u), part_d], last_d.at[:, h, both(u)], over_y
        )
        for part_of in range(2):
            q0 = quarters[part_of].start
            y2_copy[h, u, part_of].wait_recv()

            @pl.loop(q0, q0 + quarters[part_of].size)
            def _(q):
                for xx in range(2):
                    add_into(rows.at[q, xx, y, 1, h, both(u), part_a], got_y2[q, xx, h, both(u)])

        for k in pair[u]:
            if k:
                send_home(h, k, rows.at[:, :, y, 1, h, spots(k), part_a], landed_a, 0)

    def add_third(h, u):
        d_copy[h, u].wait_recv()

        @pl.loop(0, slabs)
        def _(q):
            add_into(rows.at[q, x, y, 1, h, both(u), part_d], last_d[q, h, both(u)])

        for k in pair[u]:
            if k:
                send_home(h, k, rows.at[:, x, y, 1, h, spots(k), part_d], landed_d, slabs)

    a_copy = {}

    def landed_sum(h):
        for p in others:
            copy_of(landed_a.at[p, h], landed_a.at[p, h], zk[h], zk[h] + p, core).wait_recv()

        @pl.loop(0, slabs)
        def _(q):
            for xx in range(2):
                total = rows[q, xx, y, 1, h, spots(0), part_a].astype(F32)
                for p in others:
                    total = total + landed_a[p, h, q, xx].astype(F32)
                rows[q, xx, y, 1, h, spots(0), part_a] = total.astype(BF16)

        a_copy[h] = send(rows.at[:, 1 - x, y, 1, h, spots(0), part_a], last_a.at[h], over_x)

    def output(h):
        place = slice(h * half_tok, (h + 1) * half_tok)
        for p in others:
            copy_of(
                landed_d.at[p, h], landed_d.at[p, h], zk[h], zk[h] + slabs + p, core
            ).wait_recv()
        for q in range(slabs):
            total = hidden[q, place, part_d].astype(F32)
            total = total + rows[q, x, y, 1, h, spots(0), part_d].astype(F32)
            for p in others:
                total = total + landed_d[p, h, q].astype(F32)
            out_ref[place, q * plane + cut : (q + 1) * plane] = total.astype(BF16)
        a_copy[h].wait_recv()
        for q in range(slabs):
            total = hidden[q, place, part_a].astype(F32)
            total = total + rows[q, x, y, 1, h, spots(0), part_a].astype(F32)
            total = total + last_a[h, q].astype(F32)
            out_ref[place, q * plane : q * plane + cut] = total.astype(BF16)

    first(0, 0)
    first(0, 1)
    second(0, 0)
    first(0, 2)
    gate_x.wait_recv()
    gate_y = send(gates.at[:, :, y, c], gates.at[:, :, y, c], over_y)
    second(0, 1)
    third(0, 0)
    first(0, 3)
    second(0, 2)
    gate_y.wait_recv()
    gate_c = send(gates.at[:, :, :, c], gates.at[:, :, :, c], core)
    up_project(0, 0)
    third(0, 1)
    first(1, 0)
    second(0, 3)
    up_project(0, 1)
    third(0, 2)
    first(1, 1)
    second(1, 0)
    up_project(0, 2)
    third(0, 3)
    first(1, 2)
    second(1, 1)
    third(1, 0)
    up_project(0, 3)
    clear(0)
    gate_c.wait_recv()
    first(1, 3)
    second(1, 2)
    down_project(0, 0)
    third(1, 1)
    add_cores(0, 0)
    second(1, 3)
    down_project(0, 1)
    third(1, 2)
    up_project(1, 0)
    add_cores(0, 1)
    third(1, 3)
    up_project(1, 1)
    add_second(0, 0)
    up_project(1, 2)
    add_third(0, 0)
    up_project(1, 3)
    clear(1)
    add_second(0, 1)
    down_project(1, 0)
    add_third(0, 1)
    add_cores(1, 0)
    down_project(1, 1)
    add_cores(1, 1)
    landed_sum(0)
    add_second(1, 0)
    output(0)
    add_third(1, 0)
    add_second(1, 1)
    landed_sum(1)
    add_third(1, 1)
    output(1)
    for copy in pending[:g_start] + pending[g_start + 2 * (slabs - 1) :]:
        if all(copy is not other for other in g_copy.values()):
            copy.wait_send()
    for i in range(chunks):
        chain_do(i, None, lambda copy: copy.wait_send())
        for p in others:
            chain_do(i, p, lambda copy: copy.wait_send())
    assert count[0] <= copies_max, count[0]


def layer(queries, keys, values, docs, out_proj, residual, gain, ids, weights, gate_up, down, groups):
    slabs = groups // 2
    tok, model = residual.shape
    tokens, depth = queries.shape
    plane = model // slabs
    ff, ff2 = down.shape[0], gate_up.shape[1]
    total = tok * slabs * 8
    half = slabs * tok // 2
    cut = 3 * plane // 8 // LANES * LANES
    copies_max = 240
    dma = pltpu.SemaphoreType.DMA
    vmem = pl.BlockSpec(memory_space=pltpu.VMEM)
    hbm = pl.BlockSpec(memory_space=pl.ANY)
    return pl.pallas_call(
        functools.partial(layer_kernel, slabs, copies_max),
        out_shape=jax.ShapeDtypeStruct((tok, model), BF16),
        in_specs=[hbm] * 3 + [vmem] + [hbm] * 2 + [vmem] * 3 + [hbm] * 2,
        out_specs=vmem,
        scratch_shapes=[
            pltpu.VMEM(queries.shape, BF16),
            pltpu.VMEM(keys.shape, BF16),
            pltpu.VMEM(values.shape, BF16),
            pltpu.VMEM(out_proj.shape, BF16),
            pltpu.VMEM(residual.shape, BF16),
            pltpu.VMEM((tokens, depth), BF16),
            pltpu.VMEM(out_proj.shape, BF16),
            pltpu.VMEM((slabs, tokens, depth), BF16),
            pltpu.VMEM((slabs, tok, plane), BF16),
            pltpu.VMEM((slabs, 2, 2, tok, plane), F32),
            pltpu.VMEM((slabs, 2, tok, plane), F32),
            pltpu.VMEM((slabs, tok, plane), BF16),
            pltpu.VMEM((slabs, tok, plane), BF16),
            pltpu.VMEM((slabs, 2, 2, 2, tok, LANES), BF16),
            pltpu.VMEM((slabs, 2, 2, 2, 2, half, plane), BF16),
            pltpu.VMEM((total // 2, plane), BF16),
            pltpu.VMEM((2, total // 2, LANES), F32),
            pltpu.VMEM((2, total // 2, ff2), F32),
            pltpu.VMEM((8 * tok, ff), BF16),
            pltpu.VMEM((slabs, plane, ff2), BF16),
            pltpu.VMEM((ff, model), BF16),
            pltpu.VMEM((slabs, tok, plane), BF16),
            pltpu.VMEM((slabs, 2, 2, 2, half, plane), BF16),
            pltpu.VMEM((slabs, 2, 2, half, plane - cut), BF16),
            pltpu.VMEM((slabs, 2, 2, half, cut), BF16),
            pltpu.VMEM((slabs, 2, half, plane - cut), BF16),
            pltpu.VMEM((2, slabs, tok // 2, cut), BF16),
            pltpu.VMEM((slabs, 2, slabs, 2, tok // 2, cut), BF16),
            pltpu.VMEM((slabs, 2, slabs, tok // 2, plane - cut), BF16),
            dma((slabs + 6,)),
            dma((copies_max,)),
            dma((copies_max,)),
        ],
        compiler_params=pltpu.CompilerParams(
            collective_id=0, has_side_effects=True, vmem_limit_bytes=VMEM_LIMIT
        ),
    )(queries, keys, values, docs, out_proj, residual, gain, ids, weights, gate_up, down)


def spread_gates(expert_ids, gate_weights, experts):
    gates = jnp.sum(
        jnp.where(
            expert_ids[:, :, None] == jnp.arange(experts, dtype=jnp.int32)[None, None, :],
            gate_weights[:, :, None],
            0.0,
        ),
        axis=1,
    )
    high = lax.reduce_precision(gates, 8, 7)
    low = gates - high
    pad = -(2 * experts) % LANES
    return jnp.concatenate(
        [high, low, jnp.zeros((gates.shape[0], pad), F32)], axis=1
    ).astype(BF16)


def plain_layer(head_out, out_proj, residual, gain, extra, gate_up, down, groups, tensors):
    experts = groups * tensors
    tok, model = residual.shape
    heads = lax.all_gather(head_out, "group", axis=0, tiled=True)
    part = jnp.dot(heads, out_proj, preferred_element_type=F32)
    part = part.reshape(groups, tensors, tok, part.shape[1])
    part = lax.psum_scatter(part, "tensor", scatter_dimension=1, tiled=False)
    attended = lax.all_to_all(part, "group", split_axis=0, concat_axis=2, tiled=True)
    hidden = residual.astype(F32) + attended.reshape(tok, model)
    mean_square = jnp.mean(hidden * hidden, axis=-1, keepdims=True)
    normed = (hidden * lax.rsqrt(mean_square + 1e-06) * gain).astype(BF16)
    rows = jnp.concatenate([normed, extra], axis=1)
    rows_all = lax.all_gather(rows, ("group", "tensor"), axis=0, tiled=True)
    me = lax.axis_index("group") * tensors + lax.axis_index("tensor")
    lane = jnp.arange(extra.shape[1], dtype=jnp.int32)
    picked = (lane == me) | (lane == me + experts)
    gate_col = jnp.sum(
        jnp.where(picked[None, :], rows_all[:, model:].astype(F32), 0.0), axis=1, keepdims=True
    )
    ff = down.shape[0]
    projected = jnp.dot(rows_all[:, :model], gate_up, preferred_element_type=F32)
    activated = (jax.nn.silu(projected[:, :ff]) * projected[:, ff:]).astype(BF16)
    expert_out = jnp.dot(activated, down, preferred_element_type=F32)
    weighted = (expert_out * gate_col).astype(BF16)
    expert_sum = lax.psum_scatter(weighted, ("group", "tensor"), scatter_dimension=0, tiled=True)
    return (hidden + expert_sum.astype(F32)).astype(BF16)


def on_device(
    queries,
    keys,
    values,
    document_index,
    out_proj,
    residual_in,
    norm_gain,
    expert_ids,
    gate_weights,
    w_gate_up,
    w_down,
):
    groups, tensors = lax.axis_size("group"), lax.axis_size("tensor")
    gain = norm_gain[None, :]
    if groups == 8 and tensors == 4:
        return layer(
            queries,
            keys,
            values,
            document_index,
            out_proj,
            residual_in,
            gain,
            expert_ids,
            gate_weights,
            w_gate_up[0],
            w_down[0],
            groups,
        )
    head_out = attention(queries, keys, values, document_index)
    extra = spread_gates(expert_ids, gate_weights, groups * tensors)
    return plain_layer(
        head_out, out_proj, residual_in, gain, extra, w_gate_up[0], w_down[0], groups, tensors
    )


def solution(mesh):
    in_specs = (
        P("group", "tensor"),
        P("group", "tensor"),
        P("group", "tensor"),
        P("group", None),
        P("tensor", "group"),
        P(("group", "tensor"), None),
        P(),
        P(("group", "tensor"), None),
        P(("group", "tensor"), None),
        P(("group", "tensor"), None, None),
        P(("group", "tensor"), None, None),
    )
    out_specs = P(("group", "tensor"), None)
    return jax.shard_map(
        on_device, mesh=mesh, in_specs=in_specs, out_specs=out_specs, check_vma=False
    )
```

time: 155 us -> 141 us (0.910); the launches traced: 155 us -> 139 us
  Pallas kernels: 146 us -> 135 us
  matrix products: 2.03 us -> 0 us
  other arithmetic: 1.74 us -> 0 us
    pallas_call x1, Pallas kernels: 146 us -> 135 us  [layer(): pl.pallas_call(functools.partial(layer_kernel, slabs, copies_max), out_sh...]
    dot_general x2 -> x0, matrix products: 2.03 us -> none  [the longest x1 1.04 us: attention(): jnp.einsum('grqk,kgd->qgrd', weights, value_head_split, preferred_element...]
    unnamed x5 -> x3, local copies, waits for them, and re-layouts: 3.35 us -> 4.39 us
where the time goes in v2:
time: 141 us; the launch traced here: 139 us
  Pallas kernels  135 us (96%)
  local copies, waits for them, and re-layouts  4.39 us (3%)
    pallas_call x1, Pallas kernels, layer(): pl.pallas_call(functools.partial(layer_kernel, slabs, copies_max), out_sh...  135 us
    unnamed x3, local copies, waits for them, and re-layouts  4.39 us

profile of v2, /device:TPU:0, one launch (start us, length us, event | category | flops | bytes accessed | tf_op | source)
XLA Modules:
  0.0 138.9 jit_solution(16824954645281645161)
XLA Ops:
  0.0 1.4 copy.12.ids_ref
  1.4 1.4 copy.13.weight_ref
  2.7 134.5 %shard_map.109 = bf16[32,4096]{1,0:T(8,128)(2,1)} custom-call(bf16[128,1024]{1,0:T(8,128)(2,1)} %query_hbm.1, bf16[128,128]{1,0:T(8,128)(2,1)} %key_hbm.1, bf16[128,128]{1,0:T(8,128)(2,1)} %value_hbm.1, s32[1,128]{1,0:T(1,128)} %doc_ref.1, bf16[1024,512]{1,0:T(8,128)(2,1)} %proj_hbm.1, bf16[32,4096]{1,0:T(8,128)(2,1)} %res_hbm.1, f32[1,4096]{1,0:T(1,128)} %bitcast.5, ...), custom_call_target="tpu_custom_call" | custom-call | tf_op jit(solution)/shard_map/pallas_call | solution.py:680
  137.3 1.7 %copy.15 = bf16[32,4096]{1,0:T(8,128)(2,1)} copy(bf16[32,4096]{1,0:T(8,128)(2,1)} %shard_map.109) | data formatting | bytes 524288

commit v3 on v2

--- a/solution.py
+++ b/solution.py
@@ -76,9 +76,10 @@
     got_half,
     sum_half,
     got_y,
+    ids_pad,
+    weight_pad,
     gates,
     rows,
-    scaled,
     squares,
     acc,
     act,
@@ -140,18 +141,25 @@
     ]
     loads.append(pltpu.make_async_copy(down_hbm, down, load_sem.at[slabs]))
 
-    lane = lax.broadcasted_iota(jnp.int32, (tok, LANES), 1)
-    gate = jnp.zeros((tok, LANES), F32)
-    for k in range(ids_ref.shape[1]):
-        chosen = ids_ref[:, k : k + 1]
-        hit = (lane == chosen) | (lane == chosen + experts)
-        gate = gate + jnp.where(hit, weight_ref[:, k : k + 1], 0.0)
+    ids_pad[...] = jnp.zeros_like(ids_pad)
+    weight_pad[...] = jnp.zeros_like(weight_pad)
+    ids_pad[:, :tok] = ids_ref[...]
+    weight_pad[:, :tok] = weight_ref[...]
+    expert = lax.broadcasted_iota(jnp.int32, (LANES, LANES), 0)
+    gate = jnp.zeros((LANES, LANES), F32)
+    for k in range(ids_ref.shape[0]):
+        chosen = ids_pad[k : k + 1, :]
+        hit = (expert == chosen) | (expert == chosen + experts)
+        gate = gate + jnp.where(hit, weight_pad[k : k + 1, :], 0.0)
     gate_high = gate.astype(BF16).astype(F32)
-    gates[z, x, y, c] = jnp.where(lane < experts, gate_high, gate - gate_high).astype(BF16)
+    gate = jnp.where(expert < experts, gate_high, gate - gate_high)
+    gates[z, x, y, c] = gate.T[:tok].astype(BF16)
     squares[...] = jnp.zeros_like(squares)
 
     for load in small[:3]:
         load.wait()
+    for load in loads:
+        load.start()
 
     def attend():
         tokens = query_ref.shape[0]
@@ -179,8 +187,6 @@
     for load in small[3:]:
         load.wait()
     pl.semaphore_wait(barrier, len(partners))
-    for load in loads:
-        load.start()
 
     count = [0]
     pending = []
@@ -215,11 +221,10 @@
             pending.append(copy)
         return lambda p: copy_of(target(p), target(p), k, k + p, core)
 
-    pieces = 2
-    piece = width // pieces
+    pieces = [(0, width // 2), (width // 2, width // 4), (3 * width // 4, width // 4)]
     proj_copy = []
-    for i in range(pieces):
-        cols = pl.ds(i * piece, piece)
+    for start, size in pieces:
+        cols = pl.ds(start, size)
         proj_copy.append(send(proj_ref.at[:, cols], proj_x.at[:, cols], over_x))
     above = device(jnp.minimum(z + 1, slabs - 1), x, y, c)
     below = device(jnp.maximum(z - 1, 0), x, y, c)
@@ -275,7 +280,8 @@
     def columns_of(i):
         if i == 0:
             return pl.ds(pl.multiple_of(x * width, width), width)
-        return pl.ds(pl.multiple_of((1 - x) * width + (i - 1) * piece, piece), piece)
+        start, size = pieces[i - 1]
+        return pl.ds(pl.multiple_of((1 - x) * width + start, LANES), size)
 
     half_copy, y_copy = {}, {}
 
@@ -312,21 +318,42 @@
             for h in range(2):
                 rows[z, x, y, c, h, spot, columns] = total[h * half_tok : (h + 1) * half_tok]
 
+    def fold(k):
+        loads[k].wait()
+
+        @pl.loop(0, plane // LANES)
+        def _(r):
+            start = pl.multiple_of(planes[k] * plane + r * LANES, LANES)
+            scale = jnp.broadcast_to(gain_ref[:, pl.ds(start, LANES)], (LANES, LANES)).T
+            spot = pl.ds(pl.multiple_of(r * LANES, LANES), LANES)
+            for n in range(ff2 // LANES):
+                columns = slice(n * LANES, (n + 1) * LANES)
+                value = gate_up[k, spot, columns].astype(F32) * scale
+                gate_up[k, spot, columns] = value.astype(BF16)
+
     every = tuple(range(slabs))
     project(0, proj_ref[...], columns_of(0))
     to_core(0, (0,))
-    for k in range(1, slabs):
-        relay(planes[k])
+    fold(0)
+    fold(1)
+    relay(planes[1])
+    relay(planes[2])
+    res_wait = send_planes(lambda p: res_ref.at[:, plane_cols(p)], lambda p: res_in.at[p])
+    gate_wait = send_planes(lambda p: gates.at[z, x, y, c], lambda p: gates.at[p, x, y, c])
+    for k in (1, 2):
         project(k, proj_ref[...], columns_of(0))
         to_core(0, (k,))
-    res_wait = send_planes(lambda p: res_ref.at[:, plane_cols(p)], lambda p: res_in.at[p])
-    gate_wait = send_planes(lambda p: gates.at[z, x, y, c], lambda p: gates.at[p, x, y, c])
+    fold(2)
+    fold(3)
+    relay(planes[3])
+    project(3, proj_ref[...], columns_of(0))
+    to_core(0, (3,))
     for k in range(slabs):
         over_cores(0, (k,))
-    for i in range(pieces):
+    for i, (start, size) in enumerate(pieces):
         proj_copy[i].wait_recv()
         for k in range(slabs):
-            project(k, proj_x[:, i * piece : (i + 1) * piece], columns_of(1 + i))
+            project(k, proj_x[:, start : start + size], columns_of(1 + i))
         to_core(1 + i, every)
         if i == 0:
             res_in[z] = res_ref[:, plane_cols(z)]
@@ -335,26 +362,40 @@
         res_wait(p).wait_recv()
     for k in range(slabs):
         finish(0, (k,))
-    for i in range(pieces):
+    for i in range(len(pieces)):
         finish(1 + i, every)
 
     low, high = pl.ds(0, width), pl.ds(width, width)
     g_copy = {}
-    g_start = len(pending)
-    g_marks = {}
 
     def pass_on(kind, unit, spot, target):
         g_copy[kind, unit] = send(spot, spot, target)
 
-    z_wait = [
-        send_planes(
-            lambda p, h=h: rows.at[z, x, y, c, h], lambda p, h=h: rows.at[p, x, y, c, h]
+    z_wait = {}
+
+    def send_half(h):
+        before = len(pending)
+        z_wait[h] = send_planes(
+            lambda p: rows.at[z, x, y, c, h], lambda p: rows.at[p, x, y, c, h]
         )
-        for h in range(2)
-    ]
+        for i, copy in enumerate(pending[before:]):
+            g_copy["z", (h, i)] = copy
+
     for p in others:
         gate_wait(p).wait_recv()
     gate_x = send(gates.at[:, x, y, c], gates.at[:, x, y, c], over_x)
+    gate_copy = {}
+
+    def gates_y():
+        gate_x.wait_recv()
+        gate_copy["y"] = send(gates.at[:, :, y, c], gates.at[:, :, y, c], over_y)
+
+    def gates_c():
+        gate_copy["y"].wait_recv()
+        gate_copy["c"] = send(gates.at[:, :, :, c], gates.at[:, :, :, c], core)
+
+    def gates_done():
+        gate_copy["c"].wait_recv()
 
     def first(h, k):
         p = planes[k]
@@ -364,19 +405,25 @@
         pass_on("y", (h, k), rows.at[p, x, y, c, h, :, high], over_y)
         pass_on("c", (h, k), rows.at[p, x, y, c, h], core)
 
-    def second(h, k):
+    def second_x(h, k):
         p = planes[k]
         g_copy["x", (h, k)].wait_recv()
         pass_on("xy", (h, k), rows.at[p, :, y, c, h, :, low], over_y)
         pass_on("xc", (h, k), rows.at[p, 1 - x, y, c, h, :, low], core)
+
+    def second_y(h, k):
+        p = planes[k]
         g_copy["y", (h, k)].wait_recv()
         pass_on("yx", (h, k), rows.at[p, x, :, c, h, :, high], over_x)
         pass_on("yc", (h, k), rows.at[p, x, 1 - y, c, h, :, high], core)
 
-    def third(h, k):
+    def third_x(h, k):
         p = planes[k]
         g_copy["xy", (h, k)].wait_recv()
         pass_on("xyc", (h, k), rows.at[p, :, 1 - y, c, h, :, low], core)
+
+    def third_y(h, k):
+        p = planes[k]
         g_copy["yx", (h, k)].wait_recv()
         pass_on("yxc", (h, k), rows.at[p, 1 - x, :, c, h, :, high], core)
 
@@ -387,14 +434,12 @@
         for kind in ("c", "xc", "yc", "xyc", "yxc"):
             g_copy[kind, (h, k)].wait_recv()
         p = planes[k]
-        gain_cols = plane_cols(p)
         per = block // 2 // tok
 
         @pl.loop(0, 8)
         def _(b):
-            @pl.loop(0, per)
-            def _(s):
-                spot = pl.ds(pl.multiple_of(s * tok, tok), tok)
+            for s in range(per):
+                spot = pl.ds(s * tok, tok)
                 value = rows[p, b // 4, (b // 2) % 2, b % 2, h, spot, :].astype(F32)
                 place = pl.ds(pl.multiple_of((b * per + s) * tok, tok), tok)
                 square = squares[h, place, :]
@@ -402,15 +447,12 @@
                     strip = value[:, i * LANES : (i + 1) * LANES]
                     square = square + strip * strip
                 squares[h, place, :] = square
-                scaled[place, :] = (value * gain_ref[:, gain_cols]).astype(BF16)
-
-        if h == 0:
-            loads[k].wait()
 
         @pl.loop(0, ff2 // step)
         def _(n):
             columns = pl.ds(pl.multiple_of(n * step, step), step)
-            got = jnp.dot(scaled[...], gate_up[k, :, columns], preferred_element_type=F32)
+            tokens = rows[p, :, :, :, h].reshape(half_rows, plane)
+            got = jnp.dot(tokens, gate_up[k, :, columns], preferred_element_type=F32)
             if k:
                 acc[h, :, columns] = acc[h, :, columns] + got
             else:
@@ -419,9 +461,6 @@
     me = g * 4 + t
     half_lane = lax.broadcasted_iota(jnp.int32, (half_tok, LANES), 1)
     picked = (half_lane == me) | (half_lane == me + experts)
-    halves = slabs // 2
-    quarters = [pl.ds(0, halves), pl.ds(halves, slabs - halves)]
-    pair = [(2, 3), (0, 1)]
 
     def clear(h):
         own = pl.ds(pl.multiple_of(z * half_tok, half_tok), half_tok)
@@ -430,23 +469,19 @@
         for (kind, unit), copy in g_copy.items():
             if unit[0] == h:
                 copy.wait_send()
-        for copy in pending[g_start + h * (slabs - 1) : g_start + (h + 1) * (slabs - 1)]:
-            copy.wait_send()
 
     def spots(k):
         return pl.ds(k * half_tok, half_tok)
 
-    def both(u):
-        return pl.ds(pair[u][0] * half_tok, 2 * half_tok)
-
     cut = 3 * plane // 8 // LANES * LANES
     part_a, part_d = pl.ds(0, cut), pl.ds(cut, plane - cut)
-    c_copy, x_copy, y2_copy, d_copy = {}, {}, {}, {}
-    zk = [take(2 * slabs) for _ in range(2)]
-
-    def down_project(h, u):
+    c_copy, x_copy, y2_copy, d_copy, a_copy = {}, {}, {}, {}, {}
+    zk = {(h, q): take(2 * slabs) for h in range(2) for q in range(slabs)}
+    chunk_rows = slabs * half_tok
+
+    def down_act(h):
         for cc in range(2):
-            for i, k in enumerate(pair[u]):
+            for k in range(slabs):
                 p = planes[k]
                 for xx in range(2):
                     for yy in range(2):
@@ -464,198 +499,219 @@
                         left = acc[h, place, :ff] * scale
                         right = acc[h, place, ff:] * (scale * share)
                         value = left / (1.0 + jnp.exp(-left)) * right
-                        spot = (((cc * 2 + xx) * 2 + yy) * 2 + i) * half_tok
+                        spot = ((cc * 2 + xx) * 2 + yy) * chunk_rows + k * half_tok
                         act[spot : spot + half_tok, :] = value.astype(BF16)
-        if u == 0 and h == 0:
+        if h == 0:
             loads[slabs].wait()
+
+    def down_project(h, q):
         tile = plane // 2
-        for part_of in range(2):
-
-            @pl.loop(part_of * slabs, (part_of + 1) * slabs)
-            def _(n):
-                got = jnp.dot(
-                    act[...],
-                    down[:, pl.ds(pl.multiple_of(n * tile, tile), tile)],
-                    preferred_element_type=F32,
-                ).astype(BF16)
-                columns = pl.ds(pl.multiple_of((n % 2) * tile, tile), tile)
-                for cc in range(2):
-                    for xx in range(2):
-                        for yy in range(2):
-                            spot = ((cc * 2 + xx) * 2 + yy) * tok
-                            rows[n // 2, xx, yy, 1 - cc, h, both(u), columns] = got[
-                                spot : spot + tok
-                            ]
-
-            q = quarters[part_of]
-            c_copy[h, u, part_of] = send(
-                rows.at[q, :, :, 0, h, both(u)], got_core.at[q, :, :, h, both(u)], core
-            )
-
-    def add_into(ref, other):
-        ref[...] = (ref[...].astype(F32) + other.astype(F32)).astype(BF16)
-
-    def add_cores(h, u):
-        for part_of in range(2):
-            c_copy[h, u, part_of].wait_recv()
-            q0 = quarters[part_of].start
-
-            @pl.loop(q0, q0 + quarters[part_of].size)
-            def _(q):
+
+        @pl.loop(2 * q, 2 * q + 2)
+        def _(n):
+            got = jnp.dot(
+                act[...],
+                down[:, pl.ds(pl.multiple_of(n * tile, tile), tile)],
+                preferred_element_type=F32,
+            ).astype(BF16)
+            columns = pl.ds(pl.multiple_of((n % 2) * tile, tile), tile)
+            for cc in range(2):
                 for xx in range(2):
                     for yy in range(2):
-                        add_into(
-                            rows.at[q, xx, yy, 1, h, both(u)], got_core[q, xx, yy, h, both(u)]
-                        )
-
-            q = quarters[part_of]
-            x_copy[h, u, part_of] = send(
-                rows.at[q, 1 - x, :, 1, h, both(u), part_d], got_x.at[q, :, h, both(u)], over_x
+                        spot = ((cc * 2 + xx) * 2 + yy) * chunk_rows
+                        rows[q, xx, yy, 1 - cc, h, :, columns] = got[spot : spot + chunk_rows]
+
+        c_copy[h, q] = send(rows.at[q, :, :, 0, h], got_core.at[q, :, :, h], core)
+
+    def add_into(ref, other):
+        count_rows = ref.shape[0]
+        for start in range(0, count_rows, 32):
+            spot = slice(start, start + 32)
+            ref[spot, :] = (ref[spot, :].astype(F32) + other[spot, :].astype(F32)).astype(BF16)
+
+    def add_cores(h, q):
+        c_copy[h, q].wait_recv()
+        for xx in range(2):
+            for yy in range(2):
+                add_into(rows.at[q, xx, yy, 1, h], got_core.at[q, xx, yy, h])
+        x_copy[h, q] = send(rows.at[q, 1 - x, :, 1, h, :, part_d], got_x.at[q, :, h], over_x)
+        y2_copy[h, q] = send(rows.at[q, :, 1 - y, 1, h, :, part_a], got_y2.at[q, :, h], over_y)
+
+    def send_home(h, q, source, landing, index):
+        for k in range(1, slabs):
+            copy = copy_of(
+                source(k),
+                landing.at[z, h, q],
+                zk[h, q] + index + k,
+                zk[h, q] + index + z,
+                device(planes[k], x, y, c),
             )
-            y2_copy[h, u, part_of] = send(
-                rows.at[q, :, 1 - y, 1, h, both(u), part_a], got_y2.at[q, :, h, both(u)], over_y
-            )
-
-    def send_home(h, k, src, landing, index):
-        copy = copy_of(
-            src, landing.at[z, h], zk[h] + index + k, zk[h] + index + z, device(planes[k], x, y, c)
+            copy.start()
+            pending.append(copy)
+
+    def landed(h, q, landing, index):
+        for p in others:
+            spot = landing.at[p, h, q]
+            copy_of(spot, spot, zk[h, q], zk[h, q] + index + p, core).wait_recv()
+
+    def add_a(h, q):
+        y2_copy[h, q].wait_recv()
+        for xx in range(2):
+            add_into(rows.at[q, xx, y, 1, h, :, part_a], got_y2.at[q, xx, h])
+        send_home(h, q, lambda k: rows.at[q, :, y, 1, h, spots(k), part_a], landed_a, 0)
+
+    def add_d(h, q):
+        x_copy[h, q].wait_recv()
+        for yy in range(2):
+            add_into(rows.at[q, x, yy, 1, h, :, part_d], got_x.at[q, yy, h])
+        d_copy[h, q] = send(rows.at[q, x, 1 - y, 1, h, :, part_d], last_d.at[q, h], over_y)
+
+    def add_last(h, q):
+        d_copy[h, q].wait_recv()
+        add_into(rows.at[q, x, y, 1, h, :, part_d], last_d.at[q, h])
+        send_home(h, q, lambda k: rows.at[q, x, y, 1, h, spots(k), part_d], landed_d, slabs)
+
+    def landed_sum(h, q):
+        landed(h, q, landed_a, 0)
+        for xx in range(2):
+            total = rows[q, xx, y, 1, h, spots(0), part_a].astype(F32)
+            for p in others:
+                total = total + landed_a[p, h, q, xx].astype(F32)
+            rows[q, xx, y, 1, h, spots(0), part_a] = total.astype(BF16)
+        a_copy[h, q] = send(
+            rows.at[q, 1 - x, y, 1, h, spots(0), part_a], last_a.at[h, q], over_x
         )
-        copy.start()
-        pending.append(copy)
-
-    def add_second(h, u):
-        for part_of in range(2):
-            q0 = quarters[part_of].start
-            x_copy[h, u, part_of].wait_recv()
-
-            @pl.loop(q0, q0 + quarters[part_of].size)
-            def _(q):
-                for yy in range(2):
-                    add_into(rows.at[q, x, yy, 1, h, both(u), part_d], got_x[q, yy, h, both(u)])
-
-        d_copy[h, u] = send(
-            rows.at[:, x, 1 - y, 1, h, both(u), part_d], last_d.at[:, h, both(u)], over_y
-        )
-        for part_of in range(2):
-            q0 = quarters[part_of].start
-            y2_copy[h, u, part_of].wait_recv()
-
-            @pl.loop(q0, q0 + quarters[part_of].size)
-            def _(q):
-                for xx in range(2):
-                    add_into(rows.at[q, xx, y, 1, h, both(u), part_a], got_y2[q, xx, h, both(u)])
-
-        for k in pair[u]:
-            if k:
-                send_home(h, k, rows.at[:, :, y, 1, h, spots(k), part_a], landed_a, 0)
-
-    def add_third(h, u):
-        d_copy[h, u].wait_recv()
-
-        @pl.loop(0, slabs)
-        def _(q):
-            add_into(rows.at[q, x, y, 1, h, both(u), part_d], last_d[q, h, both(u)])
-
-        for k in pair[u]:
-            if k:
-                send_home(h, k, rows.at[:, x, y, 1, h, spots(k), part_d], landed_d, slabs)
-
-    a_copy = {}
-
-    def landed_sum(h):
+
+    def output(h, q):
+        place = slice(h * half_tok, (h + 1) * half_tok)
+        landed(h, q, landed_d, slabs)
+        total = hidden[q, place, part_d].astype(F32)
+        total = total + rows[q, x, y, 1, h, spots(0), part_d].astype(F32)
         for p in others:
-            copy_of(landed_a.at[p, h], landed_a.at[p, h], zk[h], zk[h] + p, core).wait_recv()
-
-        @pl.loop(0, slabs)
-        def _(q):
-            for xx in range(2):
-                total = rows[q, xx, y, 1, h, spots(0), part_a].astype(F32)
-                for p in others:
-                    total = total + landed_a[p, h, q, xx].astype(F32)
-                rows[q, xx, y, 1, h, spots(0), part_a] = total.astype(BF16)
-
-        a_copy[h] = send(rows.at[:, 1 - x, y, 1, h, spots(0), part_a], last_a.at[h], over_x)
-
-    def output(h):
-        place = slice(h * half_tok, (h + 1) * half_tok)
-        for p in others:
-            copy_of(
-                landed_d.at[p, h], landed_d.at[p, h], zk[h], zk[h] + slabs + p, core
-            ).wait_recv()
-        for q in range(slabs):
-            total = hidden[q, place, part_d].astype(F32)
-            total = total + rows[q, x, y, 1, h, spots(0), part_d].astype(F32)
-            for p in others:
-                total = total + landed_d[p, h, q].astype(F32)
-            out_ref[place, q * plane + cut : (q + 1) * plane] = total.astype(BF16)
-        a_copy[h].wait_recv()
-        for q in range(slabs):
-            total = hidden[q, place, part_a].astype(F32)
-            total = total + rows[q, x, y, 1, h, spots(0), part_a].astype(F32)
-            total = total + last_a[h, q].astype(F32)
-            out_ref[place, q * plane : q * plane + cut] = total.astype(BF16)
-
+            total = total + landed_d[p, h, q].astype(F32)
+        out_ref[place, q * plane + cut : (q + 1) * plane] = total.astype(BF16)
+        a_copy[h, q].wait_recv()
+        total = hidden[q, place, part_a].astype(F32)
+        total = total + rows[q, x, y, 1, h, spots(0), part_a].astype(F32)
+        total = total + last_a[h, q].astype(F32)
+        out_ref[place, q * plane : q * plane + cut] = total.astype(BF16)
+
+    send_half(0)
     first(0, 0)
+    first(1, 0)
+    second_y(0, 0)
+    second_x(0, 0)
+    second_x(1, 0)
+    second_y(1, 0)
     first(0, 1)
-    second(0, 0)
+    send_half(1)
+    third_y(0, 0)
+    third_x(0, 0)
+    gates_y()
+    up_project(0, 0)
     first(0, 2)
-    gate_x.wait_recv()
-    gate_y = send(gates.at[:, :, y, c], gates.at[:, :, y, c], over_y)
-    second(0, 1)
-    third(0, 0)
+    third_y(1, 0)
+    third_x(1, 0)
+    second_x(0, 1)
+    second_y(0, 1)
     first(0, 3)
-    second(0, 2)
-    gate_y.wait_recv()
-    gate_c = send(gates.at[:, :, :, c], gates.at[:, :, :, c], core)
-    up_project(0, 0)
-    third(0, 1)
-    first(1, 0)
-    second(0, 3)
+    gates_c()
+    up_project(1, 0)
+    second_y(0, 2)
+    second_x(0, 2)
+    first(1, 1)
+    third_y(0, 1)
+    third_x(0, 1)
+    second_y(0, 3)
+    second_x(0, 3)
     up_project(0, 1)
-    third(0, 2)
-    first(1, 1)
-    second(1, 0)
+    first(1, 2)
+    third_y(0, 2)
+    third_x(0, 2)
+    second_y(1, 1)
+    second_x(1, 1)
     up_project(0, 2)
-    third(0, 3)
-    first(1, 2)
-    second(1, 1)
-    third(1, 0)
+    first(1, 3)
+    third_y(0, 3)
+    third_x(0, 3)
+    second_y(1, 2)
+    second_x(1, 2)
     up_project(0, 3)
+    gates_done()
     clear(0)
-    gate_c.wait_recv()
-    first(1, 3)
-    second(1, 2)
+    down_act(0)
+    third_x(1, 1)
+    third_y(1, 1)
     down_project(0, 0)
-    third(1, 1)
+    second_x(1, 3)
+    second_y(1, 3)
+    down_project(0, 1)
+    down_project(0, 2)
+    third_x(1, 2)
+    third_y(1, 2)
     add_cores(0, 0)
-    second(1, 3)
-    down_project(0, 1)
-    third(1, 2)
-    up_project(1, 0)
+    down_project(0, 3)
     add_cores(0, 1)
-    third(1, 3)
     up_project(1, 1)
-    add_second(0, 0)
+    third_y(1, 3)
+    third_x(1, 3)
+    add_cores(0, 2)
+    add_cores(0, 3)
     up_project(1, 2)
-    add_third(0, 0)
+    add_a(0, 0)
+    add_d(0, 0)
+    add_a(0, 1)
     up_project(1, 3)
+    add_a(0, 2)
     clear(1)
-    add_second(0, 1)
+    down_act(1)
+    add_d(0, 1)
     down_project(1, 0)
-    add_third(0, 1)
+    add_a(0, 3)
+    landed_sum(0, 0)
+    down_project(1, 1)
+    add_last(0, 0)
+    down_project(1, 2)
+    add_d(0, 2)
     add_cores(1, 0)
-    down_project(1, 1)
+    landed_sum(0, 1)
+    add_last(0, 1)
+    down_project(1, 3)
     add_cores(1, 1)
-    landed_sum(0)
-    add_second(1, 0)
-    output(0)
-    add_third(1, 0)
-    add_second(1, 1)
-    landed_sum(1)
-    add_third(1, 1)
-    output(1)
-    for copy in pending[:g_start] + pending[g_start + 2 * (slabs - 1) :]:
-        if all(copy is not other for other in g_copy.values()):
+    landed_sum(0, 2)
+    add_cores(1, 2)
+    add_d(0, 3)
+    landed_sum(0, 3)
+    add_cores(1, 3)
+    add_last(0, 2)
+    output(0, 0)
+    add_a(1, 0)
+    add_d(1, 0)
+    output(0, 1)
+    add_a(1, 1)
+    add_a(1, 2)
+    add_d(1, 1)
+    output(0, 2)
+    landed_sum(1, 0)
+    add_last(0, 3)
+    landed_sum(1, 1)
+    add_d(1, 2)
+    add_a(1, 3)
+    landed_sum(1, 2)
+    add_last(1, 0)
+    output(0, 3)
+    add_last(1, 1)
+    add_d(1, 3)
+    landed_sum(1, 3)
+    add_last(1, 2)
+    output(1, 0)
+    add_last(1, 3)
+    output(1, 1)
+    output(1, 2)
+    output(1, 3)
+    gathered = list(g_copy.values())
+    for copy in pending:
+        if all(copy is not other for other in gathered):
             copy.wait_send()
     for i in range(chunks):
         chain_do(i, None, lambda copy: copy.wait_send())
@@ -673,7 +729,7 @@
     total = tok * slabs * 8
     half = slabs * tok // 2
     cut = 3 * plane // 8 // LANES * LANES
-    copies_max = 240
+    copies_max = 300
     dma = pltpu.SemaphoreType.DMA
     vmem = pl.BlockSpec(memory_space=pltpu.VMEM)
     hbm = pl.BlockSpec(memory_space=pl.ANY)
@@ -696,12 +752,13 @@
             pltpu.VMEM((slabs, 2, tok, plane), F32),
             pltpu.VMEM((slabs, tok, plane), BF16),
             pltpu.VMEM((slabs, tok, plane), BF16),
+            pltpu.VMEM((ids.shape[0], LANES), jnp.int32),
+            pltpu.VMEM((ids.shape[0], LANES), F32),
             pltpu.VMEM((slabs, 2, 2, 2, tok, LANES), BF16),
             pltpu.VMEM((slabs, 2, 2, 2, 2, half, plane), BF16),
-            pltpu.VMEM((total // 2, plane), BF16),
             pltpu.VMEM((2, total // 2, LANES), F32),
             pltpu.VMEM((2, total // 2, ff2), F32),
-            pltpu.VMEM((8 * tok, ff), BF16),
+            pltpu.VMEM((total // 2, ff), BF16),
             pltpu.VMEM((slabs, plane, ff2), BF16),
             pltpu.VMEM((ff, model), BF16),
             pltpu.VMEM((slabs, tok, plane), BF16),
@@ -791,8 +848,8 @@
             out_proj,
             residual_in,
             gain,
-            expert_ids,
-            gate_weights,
+            expert_ids.T,
+            gate_weights.T,
             w_gate_up[0],
             w_down[0],
             groups,

time: 141 us -> 124 us (0.88); the launches traced: 139 us -> 124 us
  Pallas kernels: 135 us -> 122 us
  local copies, waits for them, and re-layouts: 4.39 us -> 1.67 us
    pallas_call x1, Pallas kernels: 135 us -> 122 us  [layer(): pl.pallas_call(functools.partial(layer_kernel, slabs, copies_max), out_sh...]
    unnamed x3 -> x1, local copies, waits for them, and re-layouts: 4.39 us -> 1.67 us
where the time goes in v3:
time: 124 us
  Pallas kernels  122 us (98%)
  local copies, waits for them, and re-layouts  1.67 us (1%)
    pallas_call x1, Pallas kernels, layer(): pl.pallas_call(functools.partial(layer_kernel, slabs, copies_max), out_sh...  122 us

profile of v3, /device:TPU:0, one launch (start us, length us, event | category | flops | bytes accessed | tf_op | source)
XLA Modules:
  0.0 123.8 jit_solution(10556267095791619927)
XLA Ops:
  0.0 122.1 %shard_map.109 = bf16[32,4096]{1,0:T(8,128)(2,1)} custom-call(bf16[128,1024]{1,0:T(8,128)(2,1)} %query_hbm.1, bf16[128,128]{1,0:T(8,128)(2,1)} %key_hbm.1, bf16[128,128]{1,0:T(8,128)(2,1)} %value_hbm.1, s32[1,128]{1,0:T(1,128)} %doc_ref.1, bf16[1024,512]{1,0:T(8,128)(2,1)} %proj_hbm.1, bf16[32,4096]{1,0:T(8,128)(2,1)} %res_hbm.1, f32[1,4096]{1,0:T(1,128)} %bitcast.7, ...), custom_call_target="tpu_custom_call" | custom-call | tf_op jit(solution)/shard_map/pallas_call | solution.py:736
  122.2 1.7 %copy.13 = bf16[32,4096]{1,0:T(8,128)(2,1)} copy(bf16[32,4096]{1,0:T(8,128)(2,1)} %shard_map.109) | data formatting | bytes 524288

commit v4 on v3

--- a/solution.py
+++ b/solution.py
@@ -51,6 +51,7 @@
 def layer_kernel(
     slabs,
     copies_max,
+    send_slots,
     query_hbm,
     key_hbm,
     value_hbm,
@@ -190,6 +191,9 @@
 
     count = [0]
     pending = []
+    clock = [0]
+    slots = []
+    lines = {}
 
     def copy_of(src, dst, send_index, recv_index, target):
         return pltpu.make_async_remote_copy(
@@ -206,20 +210,55 @@
         count[0] = k + n
         return k
 
+    class Tracked:
+        def __init__(self, src, dst, recv_index, target):
+            free = [i for i, old in enumerate(slots) if old.sent]
+            if free:
+                slot = free[0]
+            elif len(slots) < send_slots:
+                slot = len(slots)
+                slots.append(None)
+            else:
+                slot = min(range(send_slots), key=lambda i: slots[i].started)
+                slots[slot].wait_send()
+            clock[0] += 1
+            self.started, self.ended, self.sent = clock[0], None, False
+            self.index = recv_index
+            self.copy = copy_of(src, dst, slot, recv_index, target)
+            self.copy.start()
+            slots[slot] = self
+            pending.append(self)
+
+        def wait_recv(self):
+            self.copy.wait_recv()
+            clock[0] += 1
+            self.ended = clock[0]
+
+        def wait_send(self):
+            if not self.sent:
+                self.copy.wait_send()
+                self.sent = True
+
     def send(src, dst, target):
-        k = take(1)
-        copy = copy_of(src, dst, k, k, target)
-        copy.start()
-        pending.append(copy)
+        past = lines.setdefault(id(target), [])
+        index, seen = None, set()
+        answered = max([m.started for m in past if m.ended is not None], default=0)
+        for old in reversed(past):
+            if old.index in seen:
+                continue
+            seen.add(old.index)
+            if old.ended is not None and old.ended < answered:
+                index = old.index
+                break
+        copy = Tracked(src, dst, take(1) if index is None else index, target)
+        past.append(copy)
         return copy
 
     def send_planes(source, target):
         k = take(slabs)
-        for i, p in enumerate(others):
-            copy = copy_of(source(p), target(z), k + i, k + z, device(p, x, y, c))
-            copy.start()
-            pending.append(copy)
-        return lambda p: copy_of(target(p), target(p), k, k + p, core)
+        for p in others:
+            Tracked(source(p), target(z), k + z, device(p, x, y, c))
+        return lambda p: copy_of(target(p), target(p), 0, k + p, core)
 
     pieces = [(0, width // 2), (width // 2, width // 4), (3 * width // 4, width // 4)]
     proj_copy = []
@@ -229,23 +268,24 @@
     above = device(jnp.minimum(z + 1, slabs - 1), x, y, c)
     below = device(jnp.maximum(z - 1, 0), x, y, c)
     is_low, is_high = z < slabs - 1, z > 0
-    chunks = 2
+    chunks = 4
     chunk = head_own.shape[1] // chunks
-    chain = [take(slabs + 2) for _ in range(chunks)]
+    chain = [take(slabs) for _ in range(chunks)]
+    chain_sent = [send_slots + i * (slabs + 2) for i in range(chunks)]
     spans = [pl.ds(i * chunk, chunk) for i in range(chunks)]
 
     def own_copy(i, rising):
         return copy_of(
             head_own.at[:, spans[i]],
             heads.at[z, :, spans[i]],
-            chain[i] + slabs + (0 if rising else 1),
+            chain_sent[i] + slabs + (0 if rising else 1),
             chain[i] + z,
             above if rising else below,
         )
 
     def relay_copy(i, p, target):
         spot = heads.at[p, :, spans[i]]
-        return copy_of(spot, spot, chain[i] + p, chain[i] + p, target)
+        return copy_of(spot, spot, chain_sent[i] + p, chain[i] + p, target)
 
     def chain_do(i, p, act_on):
         if p is None:
@@ -332,38 +372,64 @@
                 gate_up[k, spot, columns] = value.astype(BF16)
 
     every = tuple(range(slabs))
-    project(0, proj_ref[...], columns_of(0))
-    to_core(0, (0,))
+    near = every[:-1]
+    last = every[-1:]
+    is_end = (z == 0) | (z == slabs - 1)
+
+    def piece_of(i, ks):
+        start, size = pieces[i - 1]
+        for k in ks:
+            project(k, proj_x[:, start : start + size], columns_of(i))
+        to_core(i, ks)
+
+    def own_piece(ks):
+        for k in ks:
+            project(k, proj_ref[...], columns_of(0))
+        to_core(0, ks)
+
     fold(0)
     fold(1)
+    res_in[z] = res_ref[:, plane_cols(z)]
     relay(planes[1])
     relay(planes[2])
+    own_piece(near)
+    fold(2)
+    fold(3)
+
+    @pl.when(jnp.logical_not(is_end))
+    def _():
+        relay(planes[3])
+
+    proj_copy[0].wait_recv()
+    piece_of(1, near)
+    over_cores(0, near)
+    over_cores(1, near)
     res_wait = send_planes(lambda p: res_ref.at[:, plane_cols(p)], lambda p: res_in.at[p])
     gate_wait = send_planes(lambda p: gates.at[z, x, y, c], lambda p: gates.at[p, x, y, c])
-    for k in (1, 2):
-        project(k, proj_ref[...], columns_of(0))
-        to_core(0, (k,))
-    fold(2)
-    fold(3)
-    relay(planes[3])
-    project(3, proj_ref[...], columns_of(0))
-    to_core(0, (3,))
-    for k in range(slabs):
-        over_cores(0, (k,))
-    for i, (start, size) in enumerate(pieces):
-        proj_copy[i].wait_recv()
-        for k in range(slabs):
-            project(k, proj_x[:, start : start + size], columns_of(1 + i))
-        to_core(1 + i, every)
-        if i == 0:
-            res_in[z] = res_ref[:, plane_cols(z)]
-        over_cores(1 + i, every)
+
+    @pl.when(is_end)
+    def _():
+        for i in range(chunks):
+            relay_copy(i, planes[3], above).wait_recv()
+
+    own_piece(last)
+    piece_of(1, last)
+    proj_copy[1].wait_recv()
+    piece_of(2, every)
+    over_cores(0, last)
+    over_cores(1, last)
+    over_cores(2, every)
+    proj_copy[2].wait_recv()
+    piece_of(3, every)
     for p in others:
         res_wait(p).wait_recv()
-    for k in range(slabs):
-        finish(0, (k,))
-    for i in range(len(pieces)):
-        finish(1 + i, every)
+    finish(0, near)
+    finish(1, near)
+    finish(0, last)
+    finish(1, last)
+    over_cores(3, every)
+    finish(2, every)
+    finish(3, every)
 
     low, high = pl.ds(0, width), pl.ds(width, width)
     g_copy = {}
@@ -476,7 +542,7 @@
     cut = 3 * plane // 8 // LANES * LANES
     part_a, part_d = pl.ds(0, cut), pl.ds(cut, plane - cut)
     c_copy, x_copy, y2_copy, d_copy, a_copy = {}, {}, {}, {}, {}
-    zk = {(h, q): take(2 * slabs) for h in range(2) for q in range(slabs)}
+    zk = {h: take(2 * slabs) for h in range(2)}
     chunk_rows = slabs * half_tok
 
     def down_act(h):
@@ -539,20 +605,12 @@
 
     def send_home(h, q, source, landing, index):
         for k in range(1, slabs):
-            copy = copy_of(
-                source(k),
-                landing.at[z, h, q],
-                zk[h, q] + index + k,
-                zk[h, q] + index + z,
-                device(planes[k], x, y, c),
-            )
-            copy.start()
-            pending.append(copy)
-
-    def landed(h, q, landing, index):
+            Tracked(source(k), landing.at[z, h, q], zk[h] + index + z, device(planes[k], x, y, c))
+
+    def landed(h, landing, index):
         for p in others:
-            spot = landing.at[p, h, q]
-            copy_of(spot, spot, zk[h, q], zk[h, q] + index + p, core).wait_recv()
+            spot = landing.at[p, h]
+            copy_of(spot, spot, 0, zk[h] + index + p, core).wait_recv()
 
     def add_a(h, q):
         y2_copy[h, q].wait_recv()
@@ -571,30 +629,33 @@
         add_into(rows.at[q, x, y, 1, h, :, part_d], last_d.at[q, h])
         send_home(h, q, lambda k: rows.at[q, x, y, 1, h, spots(k), part_d], landed_d, slabs)
 
-    def landed_sum(h, q):
-        landed(h, q, landed_a, 0)
-        for xx in range(2):
-            total = rows[q, xx, y, 1, h, spots(0), part_a].astype(F32)
+    def landed_sum(h):
+        landed(h, landed_a, 0)
+        for q in range(slabs):
+            for xx in range(2):
+                total = rows[q, xx, y, 1, h, spots(0), part_a].astype(F32)
+                for p in others:
+                    total = total + landed_a[p, h, q, xx].astype(F32)
+                rows[q, xx, y, 1, h, spots(0), part_a] = total.astype(BF16)
+        a_copy[h] = send(
+            rows.at[:, 1 - x, y, 1, h, spots(0), part_a], last_a.at[h], over_x
+        )
+
+    def output(h):
+        place = slice(h * half_tok, (h + 1) * half_tok)
+        a_copy[h].wait_recv()
+        for q in range(slabs):
+            total = hidden[q, place, part_a].astype(F32)
+            total = total + rows[q, x, y, 1, h, spots(0), part_a].astype(F32)
+            total = total + last_a[h, q].astype(F32)
+            out_ref[place, q * plane : q * plane + cut] = total.astype(BF16)
+        landed(h, landed_d, slabs)
+        for q in range(slabs):
+            total = hidden[q, place, part_d].astype(F32)
+            total = total + rows[q, x, y, 1, h, spots(0), part_d].astype(F32)
             for p in others:
-                total = total + landed_a[p, h, q, xx].astype(F32)
-            rows[q, xx, y, 1, h, spots(0), part_a] = total.astype(BF16)
-        a_copy[h, q] = send(
-            rows.at[q, 1 - x, y, 1, h, spots(0), part_a], last_a.at[h, q], over_x
-        )
-
-    def output(h, q):
-        place = slice(h * half_tok, (h + 1) * half_tok)
-        landed(h, q, landed_d, slabs)
-        total = hidden[q, place, part_d].astype(F32)
-        total = total + rows[q, x, y, 1, h, spots(0), part_d].astype(F32)
-        for p in others:
-            total = total + landed_d[p, h, q].astype(F32)
-        out_ref[place, q * plane + cut : (q + 1) * plane] = total.astype(BF16)
-        a_copy[h, q].wait_recv()
-        total = hidden[q, place, part_a].astype(F32)
-        total = total + rows[q, x, y, 1, h, spots(0), part_a].astype(F32)
-        total = total + last_a[h, q].astype(F32)
-        out_ref[place, q * plane : q * plane + cut] = total.astype(BF16)
+                total = total + landed_d[p, h, q].astype(F32)
+            out_ref[place, q * plane + cut : (q + 1) * plane] = total.astype(BF16)
 
     send_half(0)
     first(0, 0)
@@ -668,51 +729,37 @@
     add_d(0, 1)
     down_project(1, 0)
     add_a(0, 3)
-    landed_sum(0, 0)
     down_project(1, 1)
     add_last(0, 0)
     down_project(1, 2)
     add_d(0, 2)
     add_cores(1, 0)
-    landed_sum(0, 1)
     add_last(0, 1)
     down_project(1, 3)
     add_cores(1, 1)
-    landed_sum(0, 2)
     add_cores(1, 2)
     add_d(0, 3)
-    landed_sum(0, 3)
+    landed_sum(0)
     add_cores(1, 3)
     add_last(0, 2)
-    output(0, 0)
     add_a(1, 0)
     add_d(1, 0)
-    output(0, 1)
     add_a(1, 1)
     add_a(1, 2)
     add_d(1, 1)
-    output(0, 2)
-    landed_sum(1, 0)
     add_last(0, 3)
-    landed_sum(1, 1)
     add_d(1, 2)
     add_a(1, 3)
-    landed_sum(1, 2)
     add_last(1, 0)
-    output(0, 3)
     add_last(1, 1)
     add_d(1, 3)
-    landed_sum(1, 3)
+    landed_sum(1)
     add_last(1, 2)
-    output(1, 0)
     add_last(1, 3)
-    output(1, 1)
-    output(1, 2)
-    output(1, 3)
-    gathered = list(g_copy.values())
+    output(0)
+    output(1)
     for copy in pending:
-        if all(copy is not other for other in gathered):
-            copy.wait_send()
+        copy.wait_send()
     for i in range(chunks):
         chain_do(i, None, lambda copy: copy.wait_send())
         for p in others:
@@ -729,12 +776,13 @@
     total = tok * slabs * 8
     half = slabs * tok // 2
     cut = 3 * plane // 8 // LANES * LANES
-    copies_max = 300
+    copies_max = 88
+    send_slots = 48
     dma = pltpu.SemaphoreType.DMA
     vmem = pl.BlockSpec(memory_space=pltpu.VMEM)
     hbm = pl.BlockSpec(memory_space=pl.ANY)
     return pl.pallas_call(
-        functools.partial(layer_kernel, slabs, copies_max),
+        functools.partial(layer_kernel, slabs, copies_max, send_slots),
         out_shape=jax.ShapeDtypeStruct((tok, model), BF16),
         in_specs=[hbm] * 3 + [vmem] + [hbm] * 2 + [vmem] * 3 + [hbm] * 2,
         out_specs=vmem,
@@ -770,7 +818,7 @@
             pltpu.VMEM((slabs, 2, slabs, 2, tok // 2, cut), BF16),
             pltpu.VMEM((slabs, 2, slabs, tok // 2, plane - cut), BF16),
             dma((slabs + 6,)),
-            dma((copies_max,)),
+            dma((send_slots + 4 * (slabs + 2),)),
             dma((copies_max,)),
         ],
         compiler_params=pltpu.CompilerParams(

time: 124 us -> 120 us (0.968)
  Pallas kernels: 122 us -> 118 us
    pallas_call x1, Pallas kernels: 122 us -> 118 us  [layer(): pl.pallas_call(functools.partial(layer_kernel, slabs, copies_max, send_sl...]
where the time goes in v4:
time: 120 us
  Pallas kernels  118 us (98%)
  local copies, waits for them, and re-layouts  1.67 us (1%)
    pallas_call x1, Pallas kernels, layer(): pl.pallas_call(functools.partial(layer_kernel, slabs, copies_max, send_sl...  118 us

profile of v4, /device:TPU:0, one launch (start us, length us, event | category | flops | bytes accessed | tf_op | source)
XLA Modules:
  0.0 120.1 jit_solution(645193298667183999)
XLA Ops:
  0.0 118.4 %shard_map.109 = bf16[32,4096]{1,0:T(8,128)(2,1)} custom-call(bf16[128,1024]{1,0:T(8,128)(2,1)} %query_hbm.1, bf16[128,128]{1,0:T(8,128)(2,1)} %key_hbm.1, bf16[128,128]{1,0:T(8,128)(2,1)} %value_hbm.1, s32[1,128]{1,0:T(1,128)} %doc_ref.1, bf16[1024,512]{1,0:T(8,128)(2,1)} %proj_hbm.1, bf16[32,4096]{1,0:T(8,128)(2,1)} %res_hbm.1, f32[1,4096]{1,0:T(1,128)} %bitcast.7, ...), custom_call_target="tpu_custom_call" | custom-call | tf_op jit(solution)/shard_map/pallas_call | solution.py:784
  118.4 1.7 %copy.13 = bf16[32,4096]{1,0:T(8,128)(2,1)} copy(bf16[32,4096]{1,0:T(8,128)(2,1)} %shard_map.109) | data formatting | bytes 524288

commit v5 on v4

--- a/solution.py
+++ b/solution.py
@@ -424,10 +424,10 @@
     for p in others:
         res_wait(p).wait_recv()
     finish(0, near)
+    over_cores(3, every)
     finish(1, near)
     finish(0, last)
     finish(1, last)
-    over_cores(3, every)
     finish(2, every)
     finish(3, every)
 
@@ -604,7 +604,7 @@
         y2_copy[h, q] = send(rows.at[q, :, 1 - y, 1, h, :, part_a], got_y2.at[q, :, h], over_y)
 
     def send_home(h, q, source, landing, index):
-        for k in range(1, slabs):
+        for k in range(slabs - 1, 0, -1):
             Tracked(source(k), landing.at[z, h, q], zk[h] + index + z, device(planes[k], x, y, c))
 
     def landed(h, landing, index):
@@ -739,7 +739,6 @@
     add_cores(1, 1)
     add_cores(1, 2)
     add_d(0, 3)
-    landed_sum(0)
     add_cores(1, 3)
     add_last(0, 2)
     add_a(1, 0)
@@ -753,9 +752,10 @@
     add_last(1, 0)
     add_last(1, 1)
     add_d(1, 3)
-    landed_sum(1)
+    landed_sum(0)
     add_last(1, 2)
     add_last(1, 3)
+    landed_sum(1)
     output(0)
     output(1)
     for copy in pending:

time: 120 us -> 120 us (level)
  no operation moved by 1% of the time
where the time goes in v5:
time: 120 us
  Pallas kernels  118 us (98%)
  local copies, waits for them, and re-layouts  1.67 us (1%)
    pallas_call x1, Pallas kernels, layer(): pl.pallas_call(functools.partial(layer_kernel, slabs, copies_max, send_sl...  118 us

profile of v5, /device:TPU:0, one launch (start us, length us, event | category | flops | bytes accessed | tf_op | source)
XLA Modules:
  0.0 119.6 jit_solution(4964388845484800156)
XLA Ops:
  0.0 118.0 %shard_map.109 = bf16[32,4096]{1,0:T(8,128)(2,1)} custom-call(bf16[128,1024]{1,0:T(8,128)(2,1)} %query_hbm.1, bf16[128,128]{1,0:T(8,128)(2,1)} %key_hbm.1, bf16[128,128]{1,0:T(8,128)(2,1)} %value_hbm.1, s32[1,128]{1,0:T(1,128)} %doc_ref.1, bf16[1024,512]{1,0:T(8,128)(2,1)} %proj_hbm.1, bf16[32,4096]{1,0:T(8,128)(2,1)} %res_hbm.1, f32[1,4096]{1,0:T(1,128)} %bitcast.7, ...), custom_call_target="tpu_custom_call" | custom-call | tf_op jit(solution)/shard_map/pallas_call | solution.py:784
  118.0 1.7 %copy.13 = bf16[32,4096]{1,0:T(8,128)(2,1)} copy(bf16[32,4096]{1,0:T(8,128)(2,1)} %shard_map.109) | data formatting | bytes 524288
